TPU v7x, 128 devices: a whole 4x4x4 slice. The times are simulated.
128 devices in a mesh: sub: 16 (over x_hi, z, core), sta: 8 (over x_lo, y).
Axes of the slice: x: 4 (x_hi: 2, x_lo: 2; x = x_hi * 2 + x_lo), y: 4, z: 4, core: 2. Of those that a mesh axis runs over, the one named last changes fastest.
Arguments:
- voltages: bfloat16 [16, 2, 64, 65536], P('sub', None, 'sta'), may hold values from -6 to 6
- beam_weights: bfloat16 [16, 2, 32, 64], P('sub'), may hold values from -0.5 to 0.5
- station_delays: int32 [64], P('sta'), may hold values from 0 to 16383
- dm_index: int32 [32, 1], P('sta'), may hold values from 1 to 8
Outputs:
- dedispersed: float32 [16, 2, 32, 1, 65536], P(None, None, None, None, ('sub', 'sta'))
- intensity: float32 [32, 1, 65536], P(None, None, ('sub', 'sta'))
Inputs may be any that keep to these rules, and one draw needn't show every extreme that they name: `station_delays`: delays in whole samples. `dm_index`: dispersion measure in steps of 10.
All inputs are finite; a program needn't handle non-finite values.
Results may differ from a plain program's by a relative error of at most 0.0006.
Values may be sent and summed in bfloat16 or wider, within the bound.
No kernel may reach another device: no remote copies, remote signals or barrier semaphores. Data moves between devices by JAX's collectives and lax.ppermute only.
A program may use at most 320 MiB of HBM per device.

v0:
```python
import jax
import jax.numpy as jnp
from jax import lax
from jax.sharding import PartitionSpec as P

ROOT = 256


TWO_PI = 6.283185307179586
DISPERSION = 4148808000.0
DM_STEP = 10.0
BASE_FREQ = 120.0
CHANNEL_WIDTH = 0.1953125
HIGHEST = lax.Precision.HIGHEST


def in_blocks(array, dim, devices):
    shape = array.shape
    tiles = array.reshape(*shape[:dim], devices, shape[dim] // devices, *shape[dim + 1 :])
    return jnp.moveaxis(tiles, dim, 0)


def in_order(tiles, dim):
    shape = list(tiles.shape[1:])
    shape[dim] *= tiles.shape[0]
    return jnp.moveaxis(tiles, 0, dim).reshape(shape)


def joined_exchange(array, axis, axes, splits, concats):
    sizes = [lax.axis_size(a) for a in axes]
    tiles = in_blocks(array, splits[0], sizes[0])
    tiles = jnp.moveaxis(in_blocks(tiles, splits[1] + 1, sizes[1]), 0, 1)
    inside = tiles.shape[2:]
    tiles = tiles.reshape(-1, *inside)
    tiles = lax.all_to_all(tiles, axis, split_axis=0, concat_axis=0, tiled=True)
    tiles = in_order(tiles.reshape(*sizes, *inside), concats[0] + 1)
    return in_order(tiles, concats[1])


def angle_tables(rows_len, modulus):
    first = jnp.arange(rows_len, dtype=jnp.int32)[:, None]
    second = jnp.arange(rows_len, dtype=jnp.int32)[None, :]
    product = first * second % modulus
    angles = TWO_PI * product.astype(jnp.float32) / modulus
    return (jnp.cos(angles), jnp.sin(angles))


def chirp_base(subband, root_len, total_len):
    first = jnp.arange(root_len, dtype=jnp.int32)[:, None]
    second = jnp.arange(root_len, dtype=jnp.int32)[None, :]
    positions = first + root_len * second
    signed_bin = jnp.where(positions < total_len // 2, positions, positions - total_len)
    offset = (CHANNEL_WIDTH * signed_bin.astype(jnp.float32) / total_len)[None]
    centre = (BASE_FREQ + CHANNEL_WIDTH * (subband.astype(jnp.float32) + 0.5))[:, None, None]
    return TWO_PI * DISPERSION * offset * offset / (centre * centre * (centre + offset))


def left_dft(cos_table, sin_table, x_real, x_imag, flip_sign):
    real_part = jnp.einsum(
        "kt,...tu->...ku", cos_table, x_real, precision=HIGHEST
    ) + flip_sign * jnp.einsum("kt,...tu->...ku", sin_table, x_imag, precision=HIGHEST)
    imag_part = jnp.einsum(
        "kt,...tu->...ku", cos_table, x_imag, precision=HIGHEST
    ) - flip_sign * jnp.einsum("kt,...tu->...ku", sin_table, x_real, precision=HIGHEST)
    return (real_part, imag_part)


def right_dft(cos_table, sin_table, x_real, x_imag, flip_sign):
    real_part = jnp.einsum(
        "...kt,tm->...km", x_real, cos_table, precision=HIGHEST
    ) + flip_sign * jnp.einsum("...kt,tm->...km", x_imag, sin_table, precision=HIGHEST)
    imag_part = jnp.einsum(
        "...kt,tm->...km", x_imag, cos_table, precision=HIGHEST
    ) - flip_sign * jnp.einsum("...kt,tm->...km", x_real, sin_table, precision=HIGHEST)
    return (real_part, imag_part)


def beam_terms(w_block, v_real, v_imag):
    w_real = w_block[:, 0]
    w_imag = w_block[:, 1]
    real_part = jnp.einsum(
        "sbk,skt->bst", w_real, v_real, preferred_element_type=jnp.float32
    ) - jnp.einsum("sbk,skt->bst", w_imag, v_imag, preferred_element_type=jnp.float32)
    imag_part = jnp.einsum(
        "sbk,skt->bst", w_real, v_imag, preferred_element_type=jnp.float32
    ) + jnp.einsum("sbk,skt->bst", w_imag, v_real, preferred_element_type=jnp.float32)
    return jnp.stack([real_part, imag_part], axis=2)


def shards(voltages, beam_weights, station_delays, dm_index):
    sub_dev = voltages.shape[0]
    total_len = voltages.shape[3]
    local_beams = dm_index.shape[0]
    trials = dm_index.shape[1]
    root_len = ROOT
    doubled = jnp.concatenate([voltages, voltages], axis=3)
    shifted = jax.vmap(
        lambda rows, shift_by: lax.dynamic_slice_in_dim(rows, total_len - shift_by, total_len, 2),
        in_axes=(2, 0),
        out_axes=2,
    )(doubled, station_delays)
    own_weights = lax.dynamic_slice_in_dim(
        beam_weights, lax.axis_index("sta") * local_beams, local_beams, 2
    )
    shard_piece = lax.all_gather(shifted, "sta", axis=2, tiled=True)
    beams = beam_terms(own_weights, shard_piece[:, 0], shard_piece[:, 1])
    cos_root, sin_root = angle_tables(root_len, root_len)
    cos_twist, sin_twist = angle_tables(root_len, total_len)
    x_real = beams[:, :, 0].reshape(local_beams, sub_dev, root_len, root_len)
    x_imag = beams[:, :, 1].reshape(local_beams, sub_dev, root_len, root_len)
    a_real, a_imag = left_dft(cos_root, sin_root, x_real, x_imag, 1.0)
    b_real = a_real * cos_twist + a_imag * sin_twist
    b_imag = a_imag * cos_twist - a_real * sin_twist
    s_real, s_imag = right_dft(cos_root, sin_root, b_real, b_imag, 1.0)
    subband = lax.axis_index("sub") * sub_dev + jnp.arange(sub_dev, dtype=jnp.int32)
    base_phase = chirp_base(subband, root_len, total_len)
    dm_value = DM_STEP * dm_index.astype(jnp.float32)
    phase_table = dm_value[:, None, :, None, None] * base_phase[None, :, None, :, :]
    h_real = jnp.cos(phase_table)
    h_imag = jnp.sin(phase_table)
    c_real = s_real[:, :, None] * h_real - s_imag[:, :, None] * h_imag
    c_imag = s_real[:, :, None] * h_imag + s_imag[:, :, None] * h_real
    d_real, d_imag = right_dft(cos_root, sin_root, c_real, c_imag, -1.0)
    e_real = d_real * cos_twist - d_imag * sin_twist
    e_imag = d_imag * cos_twist + d_real * sin_twist
    scale = 1.0 / total_len
    out_real = jnp.einsum("tk,bsjku->sbjtu", cos_root, e_real, precision=HIGHEST) - jnp.einsum(
        "tk,bsjku->sbjtu", sin_root, e_imag, precision=HIGHEST
    )
    out_imag = jnp.einsum("tk,bsjku->sbjtu", cos_root, e_imag, precision=HIGHEST) + jnp.einsum(
        "tk,bsjku->sbjtu", sin_root, e_real, precision=HIGHEST
    )
    series = jnp.stack([out_real * scale, out_imag * scale], axis=1).reshape(
        sub_dev, 2, local_beams, trials, total_len
    )
    moved = joined_exchange(series, ("sub", "sta"), ("sub", "sta"), (4, 4), (0, 2))
    intensity = jnp.mean(moved[:, 0] * moved[:, 0] + moved[:, 1] * moved[:, 1], axis=0)
    return (moved, intensity)


def solution(mesh):
    return jax.shard_map(
        shards,
        mesh=mesh,
        in_specs=(
            P("sub", None, "sta", None),
            P("sub", None, None, None),
            P("sta"),
            P("sta", None),
        ),
        out_specs=(P(None, None, None, None, ("sub", "sta")), P(None, None, ("sub", "sta"))),
        check_vma=False,
    )
```

profile of v0, /device:TPU:1, one launch (start us, length us, event | category | flops | bytes accessed | tf_op | source)
XLA Modules:
  0.0 360.6 jit_solution(14308672278880408520)
XLA Ops:
  7.2 3.8 %copy.62 = bf16[1,2,8,65536]{3,1,0,2:T(2,128)(2,1)S(1)} copy(bf16[1,2,8,65536]{3,2,1,0:T(8,128)(2,1)} %param.4) | data formatting | bytes 4194304 | tf_op args[0]
  11.0 6.1 %maximum_bitcast_fusion = bf16[8,1,2,131072]{3,2,1,0:T(2,128)(2,1)} fusion(bf16[1,2,8,65536]{3,1,0,2:T(2,128)(2,1)S(1)} %copy.62), kind=kLoop, calls=%fused_computation.8 | loop fusion | flops 8388608 | bytes 6291456 | tf_op jit(solution)/shard_map/vmap()/transpose | solution.py:98
  17.1 31.3 %while.1 = (s32[]{:T(128)}, bf16[8,1,2,131072]{3,2,1,0:T(2,128)(2,1)}, s32[8,4]{0,1:T(4,128)S(1)}, bf16[8,1,2,65536]{3,2,1,0:T(2,128)(2,1)}, s32[]{:T(128)}) while((s32[]{:T(128)}, bf16[8,1,2,131072]{3,2,1,0:T(2,128)(2,1)}, s32[8,4]{0,1:T(4,128)S(1)}, bf16[8,1,2,65536]{3,2,1,0:T(2,128)(2,1)}, s32[]{:T(128)}) %tuple.26), condition=%wide.while_cond, body=%wide.while_body.sunk | while | flops 2 | bytes 525937 | solution.py:98
  17.1 0.1 constant_dynamic-slice_fusion.2
  17.2 0.6 fusion.159
  17.8 3.2 dynamic-slice_dynamic-update-slice_fusion.2
  21.0 0.1 constant_dynamic-slice_fusion.2
  21.1 0.6 fusion.159
  21.7 3.2 dynamic-slice_dynamic-update-slice_fusion.2
  24.9 0.1 constant_dynamic-slice_fusion.2
  25.0 0.6 fusion.159
  25.6 3.2 dynamic-slice_dynamic-update-slice_fusion.2
  28.8 0.1 constant_dynamic-slice_fusion.2
  28.9 0.6 fusion.159
  29.5 3.2 dynamic-slice_dynamic-update-slice_fusion.2
  32.7 0.1 constant_dynamic-slice_fusion.2
  32.8 0.6 fusion.159
  33.3 3.2 dynamic-slice_dynamic-update-slice_fusion.2
  36.6 0.1 constant_dynamic-slice_fusion.2
  36.7 0.6 fusion.159
  37.2 3.2 dynamic-slice_dynamic-update-slice_fusion.2
  40.5 0.6 fusion.159
  41.1 3.2 dynamic-slice_dynamic-update-slice_fusion.2
  44.4 0.6 fusion.159
  45.0 3.2 dynamic-slice_dynamic-update-slice_fusion.2
  48.4 4.1 %copy.119 = bf16[8,1,2,65536]{3,0,2,1:T(8,128)(2,1)} copy(bf16[8,1,2,65536]{3,2,1,0:T(2,128)(2,1)} %get-tuple-element.9) | data formatting | bytes 4194304 | tf_op jit(solution)/shard_map/vmap()/gather | solution.py:98
  52.5 1.0 fusion.66
  53.6 0.1 copy.67
  53.7 0.1 copy.70
  53.9 0.1 multiply_divide_fusion
  54.0 172.2 %all-gather.2.cloned.1.call-done = bf16[1,2,64,65536]{3,2,1,0:T(8,128)(2,1)} async-done(((bf16[1,2,8,65536]{3,2,1,0:T(8,128)(2,1)}), bf16[1,2,64,65536]{3,2,1,0:T(8,128)(2,1)}) %all-gather.2.cloned.1.call-update) | async-done | bytes 16777232 | tf_op jit(solution)/shard_map/all_gather | solution.py:105
  226.2 4.7 %fusion.1 = f32[65536,4]{0,1:T(4,128)S(1)} fusion(bf16[1,2,64,65536]{3,2,1,0:T(8,128)(2,1)} %all-gather.2.cloned.1.call-done, bf16[1,2,32,64]{3,2,1,0:T(8,128)(2,1)S(1)} %copy-done, s32[]{:T(128)S(6)} %select_n.87), kind=kOutput, calls=%fused_computation.7 | convolution fusion | flops 33554432 | bytes 9438212 | tf_op jit(solution)/shard_map/sbk,skt->bst/dot_general | solution.py:84
  231.0 5.3 %convolution_add_fusion = f32[65536,4]{0,1:T(4,128)S(1)} fusion(f32[65536,4]{0,1:T(4,128)S(1)} %fusion.1, bf16[1,2,64,65536]{3,2,1,0:T(8,128)(2,1)} %all-gather.2.cloned.1.call-done, bf16[1,2,32,64]{3,2,1,0:T(8,128)(2,1)S(1)} %copy-done, s32[]{:T(128)S(6)} %add.214, s32[]{:T(128)S(6)} %select_n.87), kind=kOutput, calls=%fused_computation.2 | convolution fusion | flops 33816576 | bytes 10486792 | tf_op jit(solution)/shard_map/sbk,skt->bst/dot_general | solution.py:86
  236.3 2.7 fusion.16
  239.0 1.2 fusion
  240.2 1.2 convolution_subtract_fusion
  241.4 2.9 fusion.20
  244.3 2.7 fusion.12
  247.1 2.7 fusion.13
  249.8 2.8 fusion.28
  252.6 2.8 fusion.24
  255.3 3.2 convolution_add_fusion.2
  258.5 2.8 convolution_subtract_fusion.2
  261.3 5.6 %fusion.51 = f32[4,256,256]{2,1,0:T(8,128)S(1)} fusion(f32[4,256,256]{2,1,0:T(8,128)S(1)} %convolution_add_fusion.2, f32[4,256,256]{2,1,0:T(8,128)S(1)} %convolution_subtract_fusion.2, f32[256,256]{1,0:T(8,128)S(1)} %multiply_divide_fusion, f32[4]{0:T(128)S(1)} %multiply_bitcast_fusion), kind=kOutput, calls=%fused_computation.83 | convolution fusion | flops 807272448 | bytes 3407888 | tf_op jit(solution)/shard_map/...kt,tm->...km/dot_general | solution.py:72
  266.9 5.8 %fusion.53 = f32[4,256,256]{2,1,0:T(8,128)S(1)} fusion(f32[4,256,256]{2,1,0:T(8,128)S(1)} %convolution_subtract_fusion.2, f32[4,256,256]{2,1,0:T(8,128)S(1)} %convolution_add_fusion.2, f32[256,256]{1,0:T(8,128)S(1)} %multiply_divide_fusion, f32[4]{0:T(128)S(1)} %multiply_bitcast_fusion), kind=kOutput, calls=%fused_computation.85 | convolution fusion | flops 807272448 | bytes 3407888 | tf_op jit(solution)/shard_map/...kt,tm->...km/dot_general | solution.py:69
  272.7 5.6 %fusion.10 = f32[4,256,256]{2,1,0:T(8,128)S(1)} fusion(f32[4,256,256]{2,1,0:T(8,128)S(1)} %fusion.51, f32[4,256,256]{2,1,0:T(8,128)S(1)} %convolution_subtract_fusion.2, f32[4,256,256]{2,1,0:T(8,128)S(1)} %convolution_add_fusion.2, f32[256,256]{1,0:T(8,128)S(1)} %multiply_divide_fusion, f32[4]{0:T(128)S(1)} %multiply_bitcast_fusion), kind=kOutput, calls=%fused_computation.25 | convolution fusion | flops 807796736 | bytes 4456464 | tf_op jit(solution)/shard_map/...kt,tm->...km/dot_general | solution.py:74
  278.4 5.9 %fusion.11 = f32[4,256,256]{2,1,0:T(8,128)S(1)} fusion(f32[4,256,256]{2,1,0:T(8,128)S(1)} %fusion.53, f32[4,256,256]{2,1,0:T(8,128)S(1)} %convolution_add_fusion.2, f32[4,256,256]{2,1,0:T(8,128)S(1)} %convolution_subtract_fusion.2, f32[256,256]{1,0:T(8,128)S(1)} %multiply_divide_fusion, f32[4]{0:T(128)S(1)} %multiply_bitcast_fusion), kind=kOutput, calls=%fused_computation.27 | convolution fusion | flops 807796736 | bytes 4456464 | tf_op jit(solution)/shard_map/...kt,tm->...km/dot_general | solution.py:71
  284.3 2.7 fusion.49
  287.0 3.7 %fusion.47 = f32[4,256,256]{2,1,0:T(8,128)} fusion(f32[4,256,256]{2,1,0:T(8,128)S(1)} %fusion.11, f32[4,256,256]{2,1,0:T(8,128)S(1)} %fusion.10, f32[256,256]{1,0:T(8,128)S(1)} %get-tuple-element.24, f32[256,256]{1,0:T(8,128)S(1)} %get-tuple-element.25), kind=kOutput, calls=%fused_computation.79 | convolution fusion | flops 807010304 | bytes 3670016 | tf_op jit(solution)/shard_map/tk,bsjku->sbjtu/dot_general | solution.py:130
  290.7 4.2 %fusion.9 = f32[1,4,1,256,256]{3,4,1,2,0:T(8,128)} fusion(f32[4,256,256]{2,1,0:T(8,128)S(1)} %fusion.49, f32[4,256,256]{2,1,0:T(8,128)S(1)} %fusion.11, f32[4,256,256]{2,1,0:T(8,128)S(1)} %fusion.10, f32[256,256]{1,0:T(8,128)S(1)} %get-tuple-element.24, f32[256,256]{1,0:T(8,128)S(1)} %get-tuple-element.25), kind=kOutput, calls=%fused_computation.23 | convolution fusion | flops 807534592 | bytes 4718592 | tf_op jit(solution)/shard_map/tk,bsjku->sbjtu/dot_general | solution.py:127
  294.9 2.5 copy.77
  297.4 2.4 stack.9
  299.8 4.9 %fusion.7 = f32[1,4,1,256,256]{3,4,1,2,0:T(8,128)} fusion(f32[4,256,256]{2,1,0:T(8,128)} %fusion.47, f32[4,256,256]{2,1,0:T(8,128)S(1)} %fusion.10, f32[4,256,256]{2,1,0:T(8,128)S(1)} %fusion.11, f32[256,256]{1,0:T(8,128)S(1)} %get-tuple-element.24, f32[256,256]{1,0:T(8,128)S(1)} %get-tuple-element.25), kind=kOutput, calls=%fused_computation.20 | convolution fusion | flops 807534592 | bytes 4718592 | tf_op jit(solution)/shard_map/tk,bsjku->sbjtu/dot_general | solution.py:130
  304.7 1.6 copy.80
  306.4 0.2 stack.10
  306.6 0.2 pad_maximum_fusion
  306.8 1.6 copy.99
  308.4 1.4 copy.81
  309.8 36.7 %all_to_all.5 = f32[128,1,2,4,1,512]{5,3,2,4,1,0:T(4,128)S(1)} all-to-all(f32[128,1,2,4,1,512]{5,3,2,4,1,0:T(4,128)S(1)} %bitcast.151), channel_id=1, replica_groups=mesh['sub'=16,'sta'=8] {'sub','sta'}, dimensions={0} | all-to-all | bytes 4194304 | tf_op jit(solution)/shard_map/all_to_all | solution.py:35
  346.5 1.2 copy.118
  347.8 1.2 copy.83
  349.0 3.5 copy.84
  352.5 0.3 fusion.23
  352.8 0.7 div.88
  (23 shorter events, 0.3 us)
Async XLA Ops:
  7.2 219.1 %copy-start = (bf16[1,2,32,64]{3,2,1,0:T(8,128)(2,1)S(1)}, bf16[1,2,32,64]{3,2,1,0:T(8,128)(2,1)}, u32[]{:S(2)}) copy-start(bf16[1,2,32,64]{3,2,1,0:T(8,128)(2,1)} %param.5) | copy-start | bytes 24580
  7.2 219.0 %all-gather.2.cloned.1.call-start = ((), (), s32[]{:S(2)}) async-start(), calls=%async_computation.1 | async-start | bytes 18874368 | tf_op jit(solution)/shard_map/all_gather | solution.py:105
  11.0 6.1 %copy-start.4 = (s32[8]{0:T(128)S(1)}, s32[8]{0:T(128)}, u32[]{:S(2)}) copy-start(s32[8]{0:T(128)} %param.6) | copy-start | bytes 100
  48.4 5.5 %copy-start.5 = (s32[4,1]{0,1:T(1,128)S(1)}, s32[4,1]{0,1:T(1,128)}, u32[]{:S(2)}) copy-start(s32[4,1]{0,1:T(1,128)} %param.7) | copy-start | bytes 52
  226.2 12.8 %copy-start.2 = (bf16[1,2,64,65536]{3,2,1,0:T(8,128)(2,1)S(1)}, bf16[1,2,64,65536]{3,2,1,0:T(8,128)(2,1)}, u32[]{:S(2)}) copy-start(bf16[1,2,64,65536]{3,2,1,0:T(8,128)(2,1)} %all-gather.2.cloned.1.call-done) | copy-start | bytes 50331652
  304.7 1.9 copy-start.3
  347.8 5.8 %copy-start.1 = (bf16[1,2,32,64]{3,2,1,0:T(8,128)(2,1)S(1)}, bf16[1,2,32,64]{3,2,1,0:T(8,128)(2,1)}, u32[]{:S(2)}) copy-start(bf16[1,2,32,64]{3,2,1,0:T(8,128)(2,1)} %param.5) | copy-start | bytes 24580
Sparse Core Ops, SparseCore 0:
  52.7 173.5 all-gather.1
where the time goes:
time: 367 us; the launch traced here: 361 us
  waiting for transfers between devices  172 us (47%)
  matrix products  73.4 us (20%)
  local copies, waits for them, and re-layouts  55.7 us (15%)
  blocking collectives  36.7 us (10%)
  between operations  14.5 us (4%)
  other arithmetic  7.77 us (2%)
    all_gather x1, waiting for transfers between devices, shards(): shard_piece = lax.all_gather(shifted, 'sta', axis=2, tiled=True)  172 us
    all_to_all x1, blocking collectives, joined_exchange(): tiles = lax.all_to_all(tiles, axis, split_axis=0, concat_axis=0, tiled=True)  36.7 us
    gather x24, local copies, waits for them, and re-layouts  31.1 us
    dot_general x2, matrix products, right_dft(): jnp.einsum('...kt,tm->...km', x_imag, sin_table, precision=HIGHEST)  9.03 us
    unnamed x16, local copies, waits for them, and re-layouts  8.91 us
    dot_general x2, matrix products, right_dft(): jnp.einsum('...kt,tm->...km', x_real, cos_table, precision=HIGHEST)  8.56 us
    dot_general x2, matrix products, right_dft(): jnp.einsum('...kt,tm->...km', x_real, sin_table, precision=HIGHEST)  8.4 us
    dot_general x2, matrix products, right_dft(): jnp.einsum('...kt,tm->...km', x_imag, cos_table, precision=HIGHEST)  8.39 us
  transfers between devices with their start and end apart: 1, of which 1 were waited for; matrix products, arithmetic and copies ran while one was open for 0% of the time, Pallas kernels for 0%

commit v1 on v0

v1 whole, which is shorter than its diff:
```python
import functools

import jax
import jax.numpy as jnp
import numpy as np
from jax import lax
from jax.experimental import pallas as pl
from jax.experimental.pallas import tpu as pltpu
from jax.sharding import PartitionSpec as P

TWO_PI = 6.283185307179586
DISPERSION = 4148808000.0
DM_STEP = 10.0
BASE_FREQ = 120.0
CHANNEL_WIDTH = 0.1953125

TOTAL = 65536
ROOT = 256
HALF = 128
LANES = 128
STA = 8
BLOCK = TOTAL // STA
TILES = BLOCK // LANES
BEAMS = 4
DEVICES = 128
CODE_STEP = 64.0
LEVELS = 32767.0
FLOOR = 1e-33

f32 = jnp.float32
bf16 = jnp.bfloat16


def split_np(table):
    high = table.astype(bf16)
    low = (table - high.astype(np.float64)).astype(bf16)
    return high, low


@functools.lru_cache(maxsize=None)
def tables():
    m = np.arange(HALF)
    fwd = []
    for parity in range(2):
        angle = 2 * np.pi * (((2 * m[:, None] + parity) * m[None, :]) % ROOT) / ROOT
        c, s = np.cos(angle), np.sin(angle)
        fwd.append(np.block([[c, s], [-s, c]]))
    fwd = np.stack(fwd)
    bwd = fwd.transpose(0, 2, 1)
    order = (2 * np.arange(64)[None, :] + np.arange(2)[:, None]).reshape(-1)
    order = np.concatenate([order, HALF + order])
    last = bwd[:, order, :]

    def left(t):
        hi, lo = split_np(t)
        return np.concatenate([hi, hi, lo], axis=2)

    def right(t):
        hi, lo = split_np(t)
        return np.concatenate([hi, hi, lo], axis=1)

    rows = np.concatenate([2 * m, 2 * m + 1])
    angle = 2 * np.pi * (rows[:, None] * np.arange(ROOT)[None, :]) / TOTAL
    twiddle = np.stack([np.cos(angle), np.sin(angle)]).astype(np.float32)
    return left(fwd), right(bwd), right(fwd), left(last), twiddle


def code_of(peak):
    return jnp.ceil(jnp.log(jnp.maximum(peak, FLOOR)) * (CODE_STEP / 0.6931471805599453)) + 1.0


def scale_of(code):
    return jnp.exp2(code * (1.0 / CODE_STEP))


def quantize(x, inverse):
    return jnp.round(x * inverse).astype(jnp.int32).astype(jnp.int16)


def widen(q):
    return q.astype(jnp.int32).astype(f32)


def shift_kernel(delay_ref, v_ref, out_ref, merged_ref):
    lane = lax.broadcasted_iota(jnp.int32, (STA, LANES), 1)
    row = lax.broadcasted_iota(jnp.int32, (STA, LANES), 0)
    fine = jnp.zeros((STA, LANES), jnp.int32)
    for q in range(STA):
        fine = jnp.where(row == q, delay_ref[q] & (LANES - 1), fine)
    index = (lane - fine) & (LANES - 1)
    keep = lane >= fine
    count = TOTAL // LANES
    wrap = 128
    picks = [row == q for q in range(STA)]

    def turned(p, j):
        x = v_ref[0, p, :, pl.ds(pl.multiple_of(j * LANES, LANES), LANES)].astype(f32)
        return jnp.take_along_axis(x, index, axis=1)

    for p in range(2):
        unroll = 8

        def fill(i, before):
            for u in range(unroll):
                j = i * unroll + u
                now = turned(p, j)
                merged_ref[wrap + j] = jnp.where(keep, now, before)
                before = now
            return before

        lax.fori_loop(0, count // unroll, fill, turned(p, count - 1))

        def front(i, carry):
            for u in range(unroll):
                merged_ref[i * unroll + u] = merged_ref[count + i * unroll + u]
            return carry

        lax.fori_loop(0, wrap // unroll, front, 0)
        starts = [wrap - lax.shift_right_logical(delay_ref[q], 7) for q in range(STA)]

        def move(i, carry):
            parts = []
            for u in range(4):
                j = i * 4 + u
                x = merged_ref[starts[0] + j]
                for q in range(1, STA):
                    x = jnp.where(picks[q], merged_ref[starts[q] + j], x)
                parts.append(x)
            wide = jnp.concatenate(parts, axis=1).astype(bf16)
            d = i // (TILES // 4)
            at = (i % (TILES // 4)) * (4 * LANES)
            out_ref[d, p, :, pl.ds(pl.multiple_of(at, 4 * LANES), 4 * LANES)] = wide
            return carry

        lax.fori_loop(0, count // 4, move, 0)


def beam_kernel(v_ref, w_ref, out_ref, sums_ref):
    w = w_ref[0].astype(f32)
    rows = []
    for d in range(STA):
        w_re = w[0, d * BEAMS : (d + 1) * BEAMS]
        w_im = w[1, d * BEAMS : (d + 1) * BEAMS]
        rows.append(jnp.concatenate([w_re, -w_im], axis=1))
        rows.append(jnp.concatenate([w_im, w_re], axis=1))
    left = jnp.concatenate(rows, axis=0).astype(bf16)
    chunk = 1024

    def mix(i, peak):
        at = pl.ds(pl.multiple_of(i * chunk, chunk), chunk)
        volts = jnp.concatenate(
            [v_ref[g, 0, :, at] for g in range(STA)] + [v_ref[g, 1, :, at] for g in range(STA)], axis=0
        )
        sums = jnp.dot(left, volts, preferred_element_type=f32)
        sums_ref[:, at] = sums
        for u in range(chunk // LANES):
            peak = jnp.maximum(peak, jnp.abs(sums[:, u * LANES : (u + 1) * LANES]))
        return peak

    peak = lax.fori_loop(0, BLOCK // chunk, mix, jnp.zeros((64, LANES), f32))
    code = code_of(peak)
    inverse = LEVELS / scale_of(code)
    for d in range(STA):
        at8 = slice(d * 8, d * 8 + 8)
        factor = inverse[at8]
        out_ref[d, :, BLOCK:] = code[at8].astype(jnp.int32).astype(jnp.int16)

        def pack(i, carry):
            at = pl.multiple_of(i * 1024, 1024)
            x = sums_ref[at8, pl.ds(at, 1024)]
            x = x * jnp.concatenate([factor] * 8, axis=1)
            out_ref[d, :, pl.ds(at, 1024)] = jnp.round(x).astype(jnp.int32).astype(jnp.int16)
            return carry

        lax.fori_loop(0, BLOCK // 1024, pack, 0)


def halves(x, axis):
    high = x.astype(bf16)
    low = (x - high.astype(f32)).astype(bf16)
    return jnp.concatenate([high, low, high], axis=axis)


QUARTER_HIGH = 1.5703125
QUARTER_MID = float(np.float32(np.round((np.pi / 2 - QUARTER_HIGH) * 2**22) / 2**22))
QUARTER_LOW = float(np.float32(np.pi / 2 - QUARTER_HIGH - QUARTER_MID))


def cos_sin(phase):
    turns = jnp.round(phase * (2 / np.pi))
    r = ((phase - turns * QUARTER_HIGH) - turns * QUARTER_MID) - turns * QUARTER_LOW
    quadrant = turns.astype(jnp.int32)
    z = r * r
    s = r + r * z * (-1.6666654611e-1 + z * (8.3321608736e-3 + z * (-1.9515295891e-4)))
    c = 1.0 - 0.5 * z + z * z * (4.166664568298827e-2 + z * (-1.388731625493765e-3 + z * 2.443315711809948e-5))
    odd = (quadrant & 1) == 1
    cos = jnp.where(odd, s, c)
    sin = jnp.where(odd, c, s)
    cos = jnp.where(((quadrant + 1) & 2) == 2, -cos, cos)
    sin = jnp.where((quadrant & 2) == 2, -sin, sin)
    return cos, sin


def dedisperse_kernel(
    sub_ref, dm_ref, x_ref, fl_ref, br_ref, fr_ref, ll_ref, tw_ref, out_ref, time_ref, base_ref, last_ref
):
    for src in range(STA):
        scale = scale_of(widen(x_ref[src, :, BLOCK:])) * (1.0 / LEVELS)

        def decode(i, carry):
            at = pl.multiple_of(i * 512, 512)
            x = widen(x_ref[src, :, pl.ds(at, 512)])
            for u in range(4):
                time_ref[src * TILES + i * 4 + u] = x[:, u * LANES : (u + 1) * LANES] * scale
            return carry

        lax.fori_loop(0, TILES // 4, decode, 0, unroll=2)

    centre = BASE_FREQ + CHANNEL_WIDTH * (sub_ref[0].astype(f32) + 0.5)
    row = lax.broadcasted_iota(jnp.int32, (ROOT, ROOT), 0)
    col = lax.broadcasted_iota(jnp.int32, (ROOT, ROOT), 1)
    k1 = 2 * (row & (HALF - 1)) + lax.shift_right_logical(row, 7)
    k2 = 2 * (col & (HALF - 1)) + lax.shift_right_logical(col, 7)
    position = k1 + ROOT * k2
    signed = jnp.where(position < TOTAL // 2, position, position - TOTAL)
    offset = CHANNEL_WIDTH * signed.astype(f32) / TOTAL
    base_ref[...] = (TWO_PI * DISPERSION) * offset * offset / (centre * centre * (centre + offset))

    flat = time_ref.reshape(TOTAL // LANES * 8, LANES)
    for b in range(BEAMS):
        x = []
        for p in range(2):
            x.append(
                jnp.concatenate([flat[pl.ds(h * 8 + p * 4 + b, ROOT, stride=16), :] for h in range(2)], axis=1)
            )
        outs = []
        for parity in range(2):
            u = [v[:HALF] + v[HALF:] if parity == 0 else v[:HALF] - v[HALF:] for v in x]
            u = jnp.concatenate(u, axis=0)
            outs.append(jnp.dot(fl_ref[parity], halves(u, 0), preferred_element_type=f32))
        re = jnp.concatenate([o[:HALF] for o in outs], axis=0)
        im = jnp.concatenate([o[HALF:] for o in outs], axis=0)
        tw_re, tw_im = tw_ref[0], tw_ref[1]
        re, im = re * tw_re + im * tw_im, im * tw_re - re * tw_im
        outs = []
        for parity in range(2):
            u = [v[:, :HALF] + v[:, HALF:] if parity == 0 else v[:, :HALF] - v[:, HALF:] for v in (re, im)]
            u = jnp.concatenate(u, axis=1)
            outs.append(jnp.dot(halves(u, 1), br_ref[parity], preferred_element_type=f32))
        measure = DM_STEP * dm_ref[b, 0].astype(f32)
        sums = []
        for parity in range(2):
            at = slice(parity * HALF, (parity + 1) * HALF)
            c, s = cos_sin(measure * base_ref[:, at])
            y_re, y_im = outs[parity][:, :HALF], outs[parity][:, HALF:]
            u = jnp.concatenate([y_re * c - y_im * s, y_re * s + y_im * c], axis=1)
            sums.append(jnp.dot(halves(u, 1), fr_ref[parity], preferred_element_type=f32))
        top, bottom = sums[0] + sums[1], sums[0] - sums[1]
        re = jnp.concatenate([top[:, :HALF], bottom[:, :HALF]], axis=1)
        im = jnp.concatenate([top[:, HALF:], bottom[:, HALF:]], axis=1)
        re, im = re * tw_re - im * tw_im, im * tw_re + re * tw_im
        sums = []
        for parity in range(2):
            at = slice(parity * HALF, (parity + 1) * HALF)
            u = jnp.concatenate([re[at], im[at]], axis=0)
            sums.append(jnp.dot(ll_ref[parity], halves(u, 0), preferred_element_type=f32))
        top = (sums[0] + sums[1]) * (1.0 / TOTAL)
        bottom = (sums[0] - sums[1]) * (1.0 / TOTAL)
        for p in range(2):
            for r in range(2):
                at = slice(p * HALF + r * 64, p * HALF + r * 64 + 64)
                for h in range(2):
                    lanes = slice(h * LANES, (h + 1) * LANES)
                    first = b * 4 + r * 2 + h
                    last_ref[p, pl.ds(first, 64, stride=16), :] = top[at, lanes]
                    last_ref[p, pl.ds(64 * 16 + first, 64, stride=16), :] = bottom[at, lanes]

    def encode(i, carry):
        for u in range(4):
            d = i * 4 + u
            at = pl.ds(pl.multiple_of(d * 16, 16), 16)
            x = [last_ref[0, at, :], last_ref[1, at, :]]
            peak = jnp.maximum(jnp.abs(x[0]), jnp.abs(x[1]))
            peak = jnp.maximum(peak[:8], peak[8:])
            code = code_of(peak)
            inverse = LEVELS / scale_of(code)
            inverse = jnp.concatenate([inverse, inverse], axis=0)
            for p in range(2):
                out_ref[d, p * 16 : p * 16 + 16, :] = quantize(x[p], inverse)
            out_ref[d, 32:40, :] = code.astype(jnp.int32).astype(jnp.int16)
        return carry

    lax.fori_loop(0, DEVICES // 4, encode, 0)


def finish_kernel(x_ref, out_ref, power_ref):
    step = pl.program_id(0)

    @pl.when(step == 0)
    def _():
        power_ref[...] = jnp.zeros_like(power_ref)

    for sta in range(STA):
        scale = scale_of(widen(x_ref[sta, 32:40, :])) * (1.0 / LEVELS)
        scale = jnp.concatenate([scale, scale], axis=0)
        re = widen(x_ref[sta, 0:16, :]) * scale
        im = widen(x_ref[sta, 16:32, :]) * scale
        out_ref[sta * 16 : sta * 16 + 16, :] = re
        out_ref[128 + sta * 16 : 128 + sta * 16 + 16, :] = im
        power_ref[sta * 16 : sta * 16 + 16, :] += re * re + im * im

    @pl.when(step == pl.num_programs(0) - 1)
    def _():
        power_ref[...] = power_ref[...] * (1.0 / 16.0)


VMEM = pl.BlockSpec(memory_space=pltpu.VMEM)
SMEM = pl.BlockSpec(memory_space=pltpu.SMEM)
PARAMS = pltpu.CompilerParams(vmem_limit_bytes=48 * 1024 * 1024)


def shift(voltages, delays):
    return pl.pallas_call(
        shift_kernel,
        out_shape=jax.ShapeDtypeStruct((STA, 2, STA, BLOCK), bf16),
        in_specs=[SMEM, VMEM],
        out_specs=VMEM,
        scratch_shapes=[pltpu.VMEM((TOTAL // LANES + 128, STA, LANES), f32)],
        compiler_params=PARAMS,
        name="shift",
    )(delays, voltages)


def beamform(volts, weights):
    return pl.pallas_call(
        beam_kernel,
        out_shape=jax.ShapeDtypeStruct((STA, 8, BLOCK + LANES), jnp.int16),
        in_specs=[VMEM, VMEM],
        out_specs=VMEM,
        scratch_shapes=[pltpu.VMEM((64, BLOCK), f32)],
        compiler_params=PARAMS,
        name="beamform",
    )(volts, weights)


def dedisperse(subband, dm_index, coded):
    fl, br, fr, ll, tw = tables()
    return pl.pallas_call(
        dedisperse_kernel,
        out_shape=jax.ShapeDtypeStruct((DEVICES, 40, LANES), jnp.int16),
        in_specs=[SMEM, SMEM] + [VMEM] * 6,
        out_specs=VMEM,
        scratch_shapes=[
            pltpu.VMEM((TOTAL // LANES, 8, LANES), f32),
            pltpu.VMEM((ROOT, ROOT), f32),
            pltpu.VMEM((2, DEVICES * 16, LANES), f32),
        ],
        compiler_params=PARAMS,
        name="dedisperse",
    )(subband, dm_index, coded, fl, br, fr, ll, tw)


def finish(coded):
    return pl.pallas_call(
        finish_kernel,
        grid=(16,),
        out_shape=(jax.ShapeDtypeStruct((4096, LANES), f32), jax.ShapeDtypeStruct((128, LANES), f32)),
        in_specs=[pl.BlockSpec((STA, 40, LANES), lambda s: (s, 0, 0))],
        out_specs=(
            pl.BlockSpec((256, LANES), lambda s: (s, 0)),
            pl.BlockSpec((128, LANES), lambda s: (0, 0)),
        ),
        compiler_params=PARAMS,
        name="finish",
    )(coded)


def shards(voltages, beam_weights, station_delays, dm_index):
    shifted = shift(voltages, station_delays)
    volts = lax.all_to_all(shifted, "sta", 0, 0, tiled=True)
    coded = beamform(volts, beam_weights)
    coded = lax.all_to_all(coded, "sta", 0, 0, tiled=True)
    subband = lax.axis_index("sub").astype(jnp.int32).reshape(1)
    coded = dedisperse(subband, dm_index, coded)
    coded = lax.all_to_all(coded, ("sub", "sta"), 0, 0, tiled=True)
    moved, intensity = finish(coded)
    return moved.reshape(16, 2, 32, 1, 512), intensity.reshape(32, 1, 512)


def solution(mesh):
    return jax.shard_map(
        shards,
        mesh=mesh,
        in_specs=(
            P("sub", None, "sta", None),
            P("sub", None, None, None),
            P("sta"),
            P("sta", None),
        ),
        out_specs=(P(None, None, None, None, ("sub", "sta")), P(None, None, ("sub", "sta"))),
        check_vma=False,
    )
```

time: 367 us -> 120 us (0.33); the launches traced: 361 us -> 119 us
  waiting for transfers between devices: 172 us -> 11.4 us
  matrix products: 73.4 us -> 0 us
  local copies, waits for them, and re-layouts: 55.7 us -> 4.53 us
  Pallas kernels: 0 us -> 33.5 us
  blocking collectives: 36.7 us -> 65.4 us
  between operations: 14.5 us -> 0.71 us
  other arithmetic: 7.77 us -> 0 us
    all_gather x1 -> x0, waiting for transfers between devices: 172 us -> none  [shards(): shard_piece = lax.all_gather(shifted, 'sta', axis=2, tiled=True)]
    dot_general x20 -> x0, matrix products: 73.4 us -> none  [the longest x2 9.03 us: right_dft(): jnp.einsum('...kt,tm->...km', x_imag, sin_table, precision=HIGHEST)]
    gather x25 -> x0, local copies, waits for them, and re-layouts: 35.2 us -> none
    pallas_call x0 -> x4, Pallas kernels: none -> 33.5 us  [the longest x1 15.3 us: shift(): pl.pallas_call(shift_kernel, out_shape=jax.ShapeDtypeStruct((STA, 2, STA,...]
    all_to_all x1 -> x2, blocking collectives: 36.7 us -> 65.4 us  [the longest x1 33.9 us: shards(): coded = lax.all_to_all(coded, ('sub', 'sta'), 0, 0, tiled=True)]
    all_to_all x0 -> x1, waiting for transfers between devices: none -> 11.4 us  [shards(): coded = lax.all_to_all(coded, 'sta', 0, 0, tiled=True)]
    transpose x1 -> x0, other arithmetic: 6.08 us -> none  [shards(): lax.dynamic_slice_in_dim(rows, total_len - shift_by, total_len, 2)]
    unnamed x16 -> x19, local copies, waits for them, and re-layouts: 8.91 us -> 4.53 us
where the time goes in v1:
time: 120 us; the launch traced here: 119 us
  blocking collectives  65.4 us (55%)
  Pallas kernels  33.5 us (28%)
  waiting for transfers between devices  11.4 us (10%)
  local copies, waits for them, and re-layouts  4.53 us (4%)
  starting transfers between devices  3.56 us (3%)
    all_to_all x1, blocking collectives, shards(): coded = lax.all_to_all(coded, ('sub', 'sta'), 0, 0, tiled=True)  33.9 us
    all_to_all x1, blocking collectives, shards(): volts = lax.all_to_all(shifted, 'sta', 0, 0, tiled=True)  31.5 us
    pallas_call x1, Pallas kernels, shift(): pl.pallas_call(shift_kernel, out_shape=jax.ShapeDtypeStruct((STA, 2, STA,...  15.3 us
    all_to_all x1, waiting for transfers between devices, shards(): coded = lax.all_to_all(coded, 'sta', 0, 0, tiled=True)  11.4 us
    pallas_call x1, Pallas kernels, dedisperse(): pl.pallas_call(dedisperse_kernel, out_shape=jax.ShapeDtypeStruct((DEVICES...  9.59 us
    pallas_call x1, Pallas kernels, finish(): pl.pallas_call(finish_kernel, grid=(16,), out_shape=(jax.ShapeDtypeStruct...  5.61 us
    unnamed x19, local copies, waits for them, and re-layouts  4.53 us
    all_to_all x1, starting transfers between devices, shards(): coded = lax.all_to_all(coded, 'sta', 0, 0, tiled=True)  3.56 us
  transfers between devices with their start and end apart: 1, of which 1 were waited for; matrix products, arithmetic and copies ran while one was open for 0% of the time, Pallas kernels for 0%

profile of v1, /device:TPU:1, one launch (start us, length us, event | category | flops | bytes accessed | tf_op | source)
XLA Modules:
  0.0 119.2 jit_solution(18286423805290044873)
XLA Ops:
  0.6 0.0 copy-start
  0.6 1.6 %copy-done = bf16[1,2,8,65536]{3,2,1,0:T(8,128)(2,1)S(1)} copy-done((bf16[1,2,8,65536]{3,2,1,0:T(8,128)(2,1)S(1)}, bf16[1,2,8,65536]{3,2,1,0:T(8,128)(2,1)}, u32[]{:S(2)}) %copy-start) | copy-done | bytes 2097176
  2.2 0.0 copy-start.7
  2.2 0.7 copy-done.7
  2.9 15.3 %shift.1 = bf16[8,2,8,8192]{3,2,1,0:T(8,128)(2,1)S(1)} custom-call(s32[8]{0:T(128)S(1)} %copy-done.7, bf16[1,2,8,65536]{3,2,1,0:T(8,128)(2,1)S(1)} %copy-done), custom_call_target="tpu_custom_call" | custom-call | tf_op jit(solution)/shard_map/shift/pallas_call | solution.py:323
  18.2 0.0 copy-start.6
  18.2 31.5 %all_to_all.15.v_ref = bf16[8,2,8,8192]{3,2,1,0:T(8,128)(2,1)S(1)} all-to-all(bf16[8,2,8,8192]{3,2,1,0:T(8,128)(2,1)S(1)} %shift.1), channel_id=1, replica_groups=mesh['sub'=16,'sta'=8] {'sta'}, dimensions={0} | all-to-all | bytes 4194304 | tf_op jit(solution)/shard_map/all_to_all | solution.py:380
  49.7 0.0 copy-done.6
  49.7 0.0 copy-start.8
  49.7 0.0 copy-start.1
  49.7 0.0 copy-start.2
  49.7 0.0 copy-start.3
  49.7 3.0 %beamform.1 = s16[8,8,8320]{2,1,0:T(8,128)(2,1)} custom-call(bf16[8,2,8,8192]{3,2,1,0:T(8,128)(2,1)S(1)} %all_to_all.15.v_ref, bf16[1,2,32,64]{3,2,1,0:T(8,128)(2,1)S(1)} %copy-done.6), custom_call_target="tpu_custom_call" | custom-call | tf_op jit(solution)/shard_map/beamform/pallas_call | solution.py:335
  52.7 3.6 %all-to-all-start.1 = ((s16[8,8,8320]{2,1,0:T(8,128)(2,1)}), s16[8,8,8320]{2,1,0:T(8,128)(2,1)S(1)}, u32[]{:S(2)}, u32[]{:S(2)}) async-start(s16[8,8,8320]{2,1,0:T(8,128)(2,1)} %beamform.1), calls=%async_computation.1 | async-start | bytes 2129920 | tf_op jit(solution)/shard_map/all_to_all | solution.py:382
  56.3 0.0 copy-done.8
  56.3 0.1 copy.11.dm_ref
  56.4 11.4 %all-to-all-done.1.x_ref = s16[8,8,8320]{2,1,0:T(8,128)(2,1)S(1)} async-done(((s16[8,8,8320]{2,1,0:T(8,128)(2,1)}), s16[8,8,8320]{2,1,0:T(8,128)(2,1)S(1)}, u32[]{:S(2)}, u32[]{:S(2)}) %all-to-all-start.1) | async-done | bytes 1064992 | tf_op jit(solution)/shard_map/all_to_all | solution.py:382
  67.8 0.0 copy-done.1
  67.8 0.0 copy-done.2
  67.8 0.0 copy-done.3
  67.9 0.0 copy-start.4
  67.9 1.1 copy-done.4
  69.0 0.0 copy-start.5
  69.0 1.0 copy-done.5
  70.0 9.6 %dedisperse.1 = s16[128,40,128]{2,1,0:T(8,128)(2,1)S(1)} custom-call(s32[1]{0:T(128)} %bitcast.sub_ref, s32[4,1]{1,0:T(4,128)S(1)} %copy.11.dm_ref, s16[8,8,8320]{2,1,0:T(8,128)(2,1)S(1)} %all-to-all-done.1.x_ref, bf16[2,256,768]{2,1,0:T(8,128)(2,1)S(1)} %copy-done.1, bf16[2,768,256]{2,1,0:T(8,128)(2,1)S(1)} %copy-done.2, ...), custom_call_target="tpu_custom_call" | custom-call | tf_op jit(solution)/shard_map/dedisperse/pallas_call | solution.py:348
  79.6 33.9 %all_to_all.16.x_ref = s16[128,40,128]{2,1,0:T(8,128)(2,1)S(1)} all-to-all(s16[128,40,128]{2,1,0:T(8,128)(2,1)S(1)} %dedisperse.1), channel_id=1, replica_groups=mesh['sub'=16,'sta'=8] {'sub','sta'}, dimensions={0} | all-to-all | bytes 2621440 | tf_op jit(solution)/shard_map/all_to_all | solution.py:385
  113.6 5.6 %finish.1 = (f32[4096,128]{1,0:T(8,128)}, f32[128,128]{1,0:T(8,128)}) custom-call(s16[128,40,128]{2,1,0:T(8,128)(2,1)S(1)} %all_to_all.16.x_ref), custom_call_target="tpu_custom_call" | custom-call | tf_op jit(solution)/shard_map/finish/pallas_call | solution.py:364
Async XLA Ops:
  0.6 1.6 %copy-start = (bf16[1,2,8,65536]{3,2,1,0:T(8,128)(2,1)S(1)}, bf16[1,2,8,65536]{3,2,1,0:T(8,128)(2,1)}, u32[]{:S(2)}) copy-start(bf16[1,2,8,65536]{3,2,1,0:T(8,128)(2,1)} %v_ref.1) | copy-start | bytes 6291460
  2.2 0.7 copy-start.7
  18.2 31.5 %copy-start.6 = (bf16[1,2,32,64]{3,2,1,0:T(8,128)(2,1)S(1)}, bf16[1,2,32,64]{3,2,1,0:T(8,128)(2,1)}, u32[]{:S(2)}) copy-start(bf16[1,2,32,64]{3,2,1,0:T(8,128)(2,1)} %w_ref.1) | copy-start | bytes 24580
  49.7 6.6 %copy-start.8 = (s32[4,1]{0,1:T(1,128)S(1)}, s32[4,1]{0,1:T(1,128)}, u32[]{:S(2)}) copy-start(s32[4,1]{0,1:T(1,128)} %param.12) | copy-start | bytes 52
  49.7 18.2 %copy-start.1 = (bf16[2,256,768]{2,1,0:T(8,128)(2,1)S(1)}, bf16[2,256,768]{2,1,0:T(8,128)(2,1)}, u32[]{:S(2)}) copy-start(bf16[2,256,768]{2,1,0:T(8,128)(2,1)} %constant.16.clone.fl_ref) | copy-start | bytes 2359300
  49.7 18.2 %copy-start.2 = (bf16[2,768,256]{2,1,0:T(8,128)(2,1)S(1)}, bf16[2,768,256]{2,1,0:T(8,128)(2,1)}, u32[]{:S(2)}) copy-start(bf16[2,768,256]{2,1,0:T(8,128)(2,1)} %constant.17.clone.br_ref) | copy-start | bytes 2359300
  49.7 18.2 %copy-start.3 = (bf16[2,768,256]{2,1,0:T(8,128)(2,1)S(1)}, bf16[2,768,256]{2,1,0:T(8,128)(2,1)}, u32[]{:S(2)}) copy-start(bf16[2,768,256]{2,1,0:T(8,128)(2,1)} %constant.18.clone.fr_ref) | copy-start | bytes 2359300
  52.7 15.1 %all-to-all-start.1 = ((s16[8,8,8320]{2,1,0:T(8,128)(2,1)}), s16[8,8,8320]{2,1,0:T(8,128)(2,1)S(1)}, u32[]{:S(2)}, u32[]{:S(2)}) async-start(s16[8,8,8320]{2,1,0:T(8,128)(2,1)} %beamform.1), calls=%async_computation.1 | async-start | bytes 2129920 | tf_op jit(solution)/shard_map/all_to_all | solution.py:382
  67.9 1.1 copy-start.4
  69.0 1.0 copy-start.5

commit v2 on v1

--- a/solution.py
+++ b/solution.py
@@ -51,18 +51,13 @@
     order = np.concatenate([order, HALF + order])
     last = bwd[:, order, :]
 
-    def left(t):
-        hi, lo = split_np(t)
-        return np.concatenate([hi, hi, lo], axis=2)
-
-    def right(t):
-        hi, lo = split_np(t)
-        return np.concatenate([hi, hi, lo], axis=1)
+    def pair(t):
+        return np.stack(split_np(t), axis=1)
 
     rows = np.concatenate([2 * m, 2 * m + 1])
     angle = 2 * np.pi * (rows[:, None] * np.arange(ROOT)[None, :]) / TOTAL
     twiddle = np.stack([np.cos(angle), np.sin(angle)]).astype(np.float32)
-    return left(fwd), right(bwd), right(fwd), left(last), twiddle
+    return pair(fwd), pair(bwd), pair(last), twiddle
 
 
 def code_of(peak):
@@ -81,58 +76,56 @@
     return q.astype(jnp.int32).astype(f32)
 
 
-def shift_kernel(delay_ref, v_ref, out_ref, merged_ref):
+FRONT = 136
+
+
+def shift_kernel(delay_ref, v_ref, out_ref, plain_ref, turned_ref):
+    count = TOTAL // LANES
     lane = lax.broadcasted_iota(jnp.int32, (STA, LANES), 1)
     row = lax.broadcasted_iota(jnp.int32, (STA, LANES), 0)
     fine = jnp.zeros((STA, LANES), jnp.int32)
     for q in range(STA):
         fine = jnp.where(row == q, delay_ref[q] & (LANES - 1), fine)
-    index = (lane - fine) & (LANES - 1)
     keep = lane >= fine
-    count = TOTAL // LANES
-    wrap = 128
-    picks = [row == q for q in range(STA)]
-
-    def turned(p, j):
-        x = v_ref[0, p, :, pl.ds(pl.multiple_of(j * LANES, LANES), LANES)].astype(f32)
-        return jnp.take_along_axis(x, index, axis=1)
-
+    source = lax.broadcasted_iota(jnp.int32, (LANES, LANES), 0)
+    target = lax.broadcasted_iota(jnp.int32, (LANES, LANES), 1)
+    turn = (target - source) & (LANES - 1)
+    unroll = 8
+    rows = count + 8
     for p in range(2):
-        unroll = 8
-
-        def fill(i, before):
+        plain = plain_ref.at[p]
+        turned = turned_ref.at[p]
+
+        def fill(i, carry):
+            at = pl.multiple_of(i * (unroll * LANES), unroll * LANES)
+            x = v_ref[0, p, :, pl.ds(at, unroll * LANES)].astype(f32)
             for u in range(unroll):
-                j = i * unroll + u
-                now = turned(p, j)
-                merged_ref[wrap + j] = jnp.where(keep, now, before)
+                to = pl.multiple_of((FRONT + i * unroll + u) * STA, STA)
+                plain[pl.ds(to, STA), :] = x[:, u * LANES : (u + 1) * LANES]
+            return carry
+
+        lax.fori_loop(0, count // unroll, fill, 0)
+        plain[: FRONT * STA, :] = plain[count * STA : (count + FRONT) * STA, :]
+        for q in range(STA):
+            fine_q = delay_ref[q] & (LANES - 1)
+            coarse_q = lax.shift_right_logical(delay_ref[q], 7)
+            matrix = (turn == fine_q).astype(f32).astype(bf16)
+            x = plain[pl.ds((FRONT - 8 - coarse_q) * STA + q, rows, stride=STA), :].astype(bf16)
+            turned[pl.ds(q, rows, stride=STA), :] = jnp.dot(x, matrix, preferred_element_type=f32)
+
+        def merge(i, before):
+            parts = []
+            for u in range(unroll):
+                now = turned[pl.ds(pl.multiple_of((8 + i * unroll + u) * STA, STA), STA), :]
+                parts.append(jnp.where(keep, now, before))
                 before = now
+            wide = jnp.concatenate(parts, axis=1).astype(bf16)
+            d = i // (TILES // unroll)
+            at = (i % (TILES // unroll)) * (unroll * LANES)
+            out_ref[d, p, :, pl.ds(pl.multiple_of(at, unroll * LANES), unroll * LANES)] = wide
             return before
 
-        lax.fori_loop(0, count // unroll, fill, turned(p, count - 1))
-
-        def front(i, carry):
-            for u in range(unroll):
-                merged_ref[i * unroll + u] = merged_ref[count + i * unroll + u]
-            return carry
-
-        lax.fori_loop(0, wrap // unroll, front, 0)
-        starts = [wrap - lax.shift_right_logical(delay_ref[q], 7) for q in range(STA)]
-
-        def move(i, carry):
-            parts = []
-            for u in range(4):
-                j = i * 4 + u
-                x = merged_ref[starts[0] + j]
-                for q in range(1, STA):
-                    x = jnp.where(picks[q], merged_ref[starts[q] + j], x)
-                parts.append(x)
-            wide = jnp.concatenate(parts, axis=1).astype(bf16)
-            d = i // (TILES // 4)
-            at = (i % (TILES // 4)) * (4 * LANES)
-            out_ref[d, p, :, pl.ds(pl.multiple_of(at, 4 * LANES), 4 * LANES)] = wide
-            return carry
-
-        lax.fori_loop(0, count // 4, move, 0)
+        lax.fori_loop(0, count // unroll, merge, turned[7 * STA : 8 * STA, :])
 
 
 def beam_kernel(v_ref, w_ref, out_ref, sums_ref):
@@ -179,6 +172,16 @@
     high = x.astype(bf16)
     low = (x - high.astype(f32)).astype(bf16)
     return jnp.concatenate([high, low, high], axis=axis)
+
+
+def dot_left(table_ref, parity, u):
+    high, low = table_ref[parity, 0], table_ref[parity, 1]
+    return jnp.dot(jnp.concatenate([high, high, low], axis=1), halves(u, 0), preferred_element_type=f32)
+
+
+def dot_right(u, table_ref, parity):
+    high, low = table_ref[parity, 0], table_ref[parity, 1]
+    return jnp.dot(halves(u, 1), jnp.concatenate([high, high, low], axis=0), preferred_element_type=f32)
 
 
 QUARTER_HIGH = 1.5703125
@@ -202,7 +205,7 @@
 
 
 def dedisperse_kernel(
-    sub_ref, dm_ref, x_ref, fl_ref, br_ref, fr_ref, ll_ref, tw_ref, out_ref, time_ref, base_ref, last_ref
+    sub_ref, dm_ref, x_ref, fwd_ref, bwd_ref, end_ref, tw_ref, out_ref, time_ref, base_ref, last_ref
 ):
     for src in range(STA):
         scale = scale_of(widen(x_ref[src, :, BLOCK:])) * (1.0 / LEVELS)
@@ -237,7 +240,7 @@
         for parity in range(2):
             u = [v[:HALF] + v[HALF:] if parity == 0 else v[:HALF] - v[HALF:] for v in x]
             u = jnp.concatenate(u, axis=0)
-            outs.append(jnp.dot(fl_ref[parity], halves(u, 0), preferred_element_type=f32))
+            outs.append(dot_left(fwd_ref, parity, u))
         re = jnp.concatenate([o[:HALF] for o in outs], axis=0)
         im = jnp.concatenate([o[HALF:] for o in outs], axis=0)
         tw_re, tw_im = tw_ref[0], tw_ref[1]
@@ -246,7 +249,7 @@
         for parity in range(2):
             u = [v[:, :HALF] + v[:, HALF:] if parity == 0 else v[:, :HALF] - v[:, HALF:] for v in (re, im)]
             u = jnp.concatenate(u, axis=1)
-            outs.append(jnp.dot(halves(u, 1), br_ref[parity], preferred_element_type=f32))
+            outs.append(dot_right(u, bwd_ref, parity))
         measure = DM_STEP * dm_ref[b, 0].astype(f32)
         sums = []
         for parity in range(2):
@@ -254,7 +257,7 @@
             c, s = cos_sin(measure * base_ref[:, at])
             y_re, y_im = outs[parity][:, :HALF], outs[parity][:, HALF:]
             u = jnp.concatenate([y_re * c - y_im * s, y_re * s + y_im * c], axis=1)
-            sums.append(jnp.dot(halves(u, 1), fr_ref[parity], preferred_element_type=f32))
+            sums.append(dot_right(u, fwd_ref, parity))
         top, bottom = sums[0] + sums[1], sums[0] - sums[1]
         re = jnp.concatenate([top[:, :HALF], bottom[:, :HALF]], axis=1)
         im = jnp.concatenate([top[:, HALF:], bottom[:, HALF:]], axis=1)
@@ -263,7 +266,7 @@
         for parity in range(2):
             at = slice(parity * HALF, (parity + 1) * HALF)
             u = jnp.concatenate([re[at], im[at]], axis=0)
-            sums.append(jnp.dot(ll_ref[parity], halves(u, 0), preferred_element_type=f32))
+            sums.append(dot_left(end_ref, parity, u))
         top = (sums[0] + sums[1]) * (1.0 / TOTAL)
         bottom = (sums[0] - sums[1]) * (1.0 / TOTAL)
         for p in range(2):
@@ -293,6 +296,9 @@
     lax.fori_loop(0, DEVICES // 4, encode, 0)
 
 
+SUBS = 4
+
+
 def finish_kernel(x_ref, out_ref, power_ref):
     step = pl.program_id(0)
 
@@ -301,13 +307,18 @@
         power_ref[...] = jnp.zeros_like(power_ref)
 
     for sta in range(STA):
-        scale = scale_of(widen(x_ref[sta, 32:40, :])) * (1.0 / LEVELS)
-        scale = jnp.concatenate([scale, scale], axis=0)
-        re = widen(x_ref[sta, 0:16, :]) * scale
-        im = widen(x_ref[sta, 16:32, :]) * scale
-        out_ref[sta * 16 : sta * 16 + 16, :] = re
-        out_ref[128 + sta * 16 : 128 + sta * 16 + 16, :] = im
-        power_ref[sta * 16 : sta * 16 + 16, :] += re * re + im * im
+        power = power_ref[sta * 16 : sta * 16 + 16, :]
+        for sub in range(SUBS):
+            src = sub * STA + sta
+            to = sub * 256 + sta * 16
+            scale = scale_of(widen(x_ref[src, 32:40, :])) * (1.0 / LEVELS)
+            scale = jnp.concatenate([scale, scale], axis=0)
+            re = widen(x_ref[src, 0:16, :]) * scale
+            im = widen(x_ref[src, 16:32, :]) * scale
+            out_ref[to : to + 16, :] = re
+            out_ref[to + 128 : to + 144, :] = im
+            power = power + (re * re + im * im)
+        power_ref[sta * 16 : sta * 16 + 16, :] = power
 
     @pl.when(step == pl.num_programs(0) - 1)
     def _():
@@ -325,7 +336,10 @@
         out_shape=jax.ShapeDtypeStruct((STA, 2, STA, BLOCK), bf16),
         in_specs=[SMEM, VMEM],
         out_specs=VMEM,
-        scratch_shapes=[pltpu.VMEM((TOTAL // LANES + 128, STA, LANES), f32)],
+        scratch_shapes=[
+            pltpu.VMEM((2, (TOTAL // LANES + FRONT) * STA, LANES), f32),
+            pltpu.VMEM((2, (TOTAL // LANES + 8) * STA, LANES), f32),
+        ],
         compiler_params=PARAMS,
         name="shift",
     )(delays, voltages)
@@ -344,11 +358,11 @@
 
 
 def dedisperse(subband, dm_index, coded):
-    fl, br, fr, ll, tw = tables()
+    fwd, bwd, end, tw = tables()
     return pl.pallas_call(
         dedisperse_kernel,
         out_shape=jax.ShapeDtypeStruct((DEVICES, 40, LANES), jnp.int16),
-        in_specs=[SMEM, SMEM] + [VMEM] * 6,
+        in_specs=[SMEM, SMEM] + [VMEM] * 5,
         out_specs=VMEM,
         scratch_shapes=[
             pltpu.VMEM((TOTAL // LANES, 8, LANES), f32),
@@ -357,17 +371,17 @@
         ],
         compiler_params=PARAMS,
         name="dedisperse",
-    )(subband, dm_index, coded, fl, br, fr, ll, tw)
+    )(subband, dm_index, coded, fwd, bwd, end, tw)
 
 
 def finish(coded):
     return pl.pallas_call(
         finish_kernel,
-        grid=(16,),
+        grid=(16 // SUBS,),
         out_shape=(jax.ShapeDtypeStruct((4096, LANES), f32), jax.ShapeDtypeStruct((128, LANES), f32)),
-        in_specs=[pl.BlockSpec((STA, 40, LANES), lambda s: (s, 0, 0))],
+        in_specs=[pl.BlockSpec((SUBS * STA, 40, LANES), lambda s: (s, 0, 0))],
         out_specs=(
-            pl.BlockSpec((256, LANES), lambda s: (s, 0)),
+            pl.BlockSpec((SUBS * 256, LANES), lambda s: (s, 0)),
             pl.BlockSpec((128, LANES), lambda s: (0, 0)),
         ),
         compiler_params=PARAMS,

time: 120 us -> 103 us (0.86)
  Pallas kernels: 33.5 us -> 19 us
  local copies, waits for them, and re-layouts: 4.53 us -> 2.36 us
    pallas_call x1, Pallas kernels: 15.3 us -> 4.55 us  [shift(): pl.pallas_call(shift_kernel, out_shape=jax.ShapeDtypeStruct((STA, 2, STA,...]
    pallas_call x1, Pallas kernels: 5.61 us -> 2 us  [finish(): pl.pallas_call(finish_kernel, grid=(16 // SUBS,), out_shape=(jax.ShapeDty...]
    unnamed x19 -> x17, local copies, waits for them, and re-layouts: 4.53 us -> 2.36 us
where the time goes in v2:
time: 103 us
  blocking collectives  65.4 us (63%)
  Pallas kernels  19 us (18%)
  waiting for transfers between devices  11.4 us (11%)
  starting transfers between devices  3.56 us (3%)
  local copies, waits for them, and re-layouts  2.36 us (2%)
    all_to_all x1, blocking collectives, shards(): coded = lax.all_to_all(coded, ('sub', 'sta'), 0, 0, tiled=True)  34 us
    all_to_all x1, blocking collectives, shards(): volts = lax.all_to_all(shifted, 'sta', 0, 0, tiled=True)  31.5 us
    all_to_all x1, waiting for transfers between devices, shards(): coded = lax.all_to_all(coded, 'sta', 0, 0, tiled=True)  11.4 us
    pallas_call x1, Pallas kernels, dedisperse(): pl.pallas_call(dedisperse_kernel, out_shape=jax.ShapeDtypeStruct((DEVICES...  9.45 us
    pallas_call x1, Pallas kernels, shift(): pl.pallas_call(shift_kernel, out_shape=jax.ShapeDtypeStruct((STA, 2, STA,...  4.55 us
    all_to_all x1, starting transfers between devices, shards(): coded = lax.all_to_all(coded, 'sta', 0, 0, tiled=True)  3.56 us
    pallas_call x1, Pallas kernels, beamform(): pl.pallas_call(beam_kernel, out_shape=jax.ShapeDtypeStruct((STA, 8, BLOCK...  3.03 us
    unnamed x17, local copies, waits for them, and re-layouts  2.36 us
  transfers between devices with their start and end apart: 1, of which 1 were waited for; matrix products, arithmetic and copies ran while one was open for 0% of the time, Pallas kernels for 0%

profile of v2, /device:TPU:1, one launch (start us, length us, event | category | flops | bytes accessed | tf_op | source)
XLA Modules:
  0.0 102.5 jit_solution(4700287195526638040)
XLA Ops:
  0.6 0.0 copy-start
  0.6 1.6 %copy-done = bf16[1,2,8,65536]{3,2,1,0:T(8,128)(2,1)S(1)} copy-done((bf16[1,2,8,65536]{3,2,1,0:T(8,128)(2,1)S(1)}, bf16[1,2,8,65536]{3,2,1,0:T(8,128)(2,1)}, u32[]{:S(2)}) %copy-start) | copy-done | bytes 2097176
  2.2 0.0 copy-start.6
  2.2 0.7 copy-done.6
  2.9 4.5 %shift.1 = bf16[8,2,8,8192]{3,2,1,0:T(8,128)(2,1)S(1)} custom-call(s32[8]{0:T(128)S(1)} %copy-done.6, bf16[1,2,8,65536]{3,2,1,0:T(8,128)(2,1)S(1)} %copy-done), custom_call_target="tpu_custom_call" | custom-call | tf_op jit(solution)/shard_map/shift/pallas_call | solution.py:334
  7.4 0.0 copy-start.5
  7.4 31.5 %all_to_all.15.v_ref = bf16[8,2,8,8192]{3,2,1,0:T(8,128)(2,1)S(1)} all-to-all(bf16[8,2,8,8192]{3,2,1,0:T(8,128)(2,1)S(1)} %shift.1), channel_id=1, replica_groups=mesh['sub'=16,'sta'=8] {'sta'}, dimensions={0} | all-to-all | bytes 4194304 | tf_op jit(solution)/shard_map/all_to_all | solution.py:394
  38.9 0.0 copy-done.5
  38.9 0.0 copy-start.7
  38.9 0.0 copy-start.1
  38.9 0.0 copy-start.2
  38.9 0.0 copy-start.3
  39.0 0.0 copy-start.4
  39.0 3.0 %beamform.1 = s16[8,8,8320]{2,1,0:T(8,128)(2,1)} custom-call(bf16[8,2,8,8192]{3,2,1,0:T(8,128)(2,1)S(1)} %all_to_all.15.v_ref, bf16[1,2,32,64]{3,2,1,0:T(8,128)(2,1)S(1)} %copy-done.5), custom_call_target="tpu_custom_call" | custom-call | tf_op jit(solution)/shard_map/beamform/pallas_call | solution.py:349
  42.0 3.6 %all-to-all-start.1 = ((s16[8,8,8320]{2,1,0:T(8,128)(2,1)}), s16[8,8,8320]{2,1,0:T(8,128)(2,1)S(1)}, u32[]{:S(2)}, u32[]{:S(2)}) async-start(s16[8,8,8320]{2,1,0:T(8,128)(2,1)} %beamform.1), calls=%async_computation.1 | async-start | bytes 2129920 | tf_op jit(solution)/shard_map/all_to_all | solution.py:396
  45.6 0.0 copy-done.7
  45.6 0.1 copy.10.dm_ref
  45.7 11.4 %all-to-all-done.1.x_ref = s16[8,8,8320]{2,1,0:T(8,128)(2,1)S(1)} async-done(((s16[8,8,8320]{2,1,0:T(8,128)(2,1)}), s16[8,8,8320]{2,1,0:T(8,128)(2,1)S(1)}, u32[]{:S(2)}, u32[]{:S(2)}) %all-to-all-start.1) | async-done | bytes 1064992 | tf_op jit(solution)/shard_map/all_to_all | solution.py:396
  57.1 0.0 copy-done.1
  57.1 0.0 copy-done.2
  57.1 0.0 copy-done.3
  57.1 0.0 copy-done.4
  57.1 9.4 %dedisperse.1 = s16[128,40,128]{2,1,0:T(8,128)(2,1)S(1)} custom-call(s32[1]{0:T(128)} %bitcast.sub_ref, s32[4,1]{1,0:T(4,128)S(1)} %copy.10.dm_ref, s16[8,8,8320]{2,1,0:T(8,128)(2,1)S(1)} %all-to-all-done.1.x_ref, bf16[2,2,256,256]{3,2,1,0:T(8,128)(2,1)S(1)} %copy-done.1, bf16[2,2,256,256]{3,2,1,0:T(8,128)(2,1)S(1)} %copy-done.2, ...), custom_call_target="tpu_custom_call" | custom-call | tf_op jit(solution)/shard_map/dedisperse/pallas_call | solution.py:362
  66.6 34.0 %all_to_all.16.x_ref = s16[128,40,128]{2,1,0:T(8,128)(2,1)S(1)} all-to-all(s16[128,40,128]{2,1,0:T(8,128)(2,1)S(1)} %dedisperse.1), channel_id=1, replica_groups=mesh['sub'=16,'sta'=8] {'sub','sta'}, dimensions={0} | all-to-all | bytes 2621440 | tf_op jit(solution)/shard_map/all_to_all | solution.py:399
  100.5 2.0 %finish.1 = (f32[4096,128]{1,0:T(8,128)}, f32[128,128]{1,0:T(8,128)}) custom-call(s16[128,40,128]{2,1,0:T(8,128)(2,1)S(1)} %all_to_all.16.x_ref), custom_call_target="tpu_custom_call" | custom-call | tf_op jit(solution)/shard_map/finish/pallas_call | solution.py:378
Async XLA Ops:
  0.6 1.6 %copy-start = (bf16[1,2,8,65536]{3,2,1,0:T(8,128)(2,1)S(1)}, bf16[1,2,8,65536]{3,2,1,0:T(8,128)(2,1)}, u32[]{:S(2)}) copy-start(bf16[1,2,8,65536]{3,2,1,0:T(8,128)(2,1)} %v_ref.1) | copy-start | bytes 6291460
  2.2 0.7 copy-start.6
  7.4 31.5 %copy-start.5 = (bf16[1,2,32,64]{3,2,1,0:T(8,128)(2,1)S(1)}, bf16[1,2,32,64]{3,2,1,0:T(8,128)(2,1)}, u32[]{:S(2)}) copy-start(bf16[1,2,32,64]{3,2,1,0:T(8,128)(2,1)} %w_ref.1) | copy-start | bytes 24580
  38.9 6.6 %copy-start.7 = (s32[4,1]{0,1:T(1,128)S(1)}, s32[4,1]{0,1:T(1,128)}, u32[]{:S(2)}) copy-start(s32[4,1]{0,1:T(1,128)} %param.11) | copy-start | bytes 52
  38.9 18.2 %copy-start.1 = (bf16[2,2,256,256]{3,2,1,0:T(8,128)(2,1)S(1)}, bf16[2,2,256,256]{3,2,1,0:T(8,128)(2,1)}, u32[]{:S(2)}) copy-start(bf16[2,2,256,256]{3,2,1,0:T(8,128)(2,1)} %constant.14.clone.fwd_ref) | copy-start | bytes 1572868
  38.9 18.2 %copy-start.2 = (bf16[2,2,256,256]{3,2,1,0:T(8,128)(2,1)S(1)}, bf16[2,2,256,256]{3,2,1,0:T(8,128)(2,1)}, u32[]{:S(2)}) copy-start(bf16[2,2,256,256]{3,2,1,0:T(8,128)(2,1)} %constant.15.clone.bwd_ref) | copy-start | bytes 1572868
  38.9 18.2 %copy-start.3 = (bf16[2,2,256,256]{3,2,1,0:T(8,128)(2,1)S(1)}, bf16[2,2,256,256]{3,2,1,0:T(8,128)(2,1)}, u32[]{:S(2)}) copy-start(bf16[2,2,256,256]{3,2,1,0:T(8,128)(2,1)} %constant.16.clone.end_ref) | copy-start | bytes 1572868
  39.0 18.2 %copy-start.4 = (f32[2,256,256]{2,1,0:T(8,128)S(1)}, f32[2,256,256]{2,1,0:T(8,128)}, u32[]{:S(2)}) copy-start(f32[2,256,256]{2,1,0:T(8,128)} %constant.17.clone.tw_ref) | copy-start | bytes 1572868
  42.0 15.1 %all-to-all-start.1 = ((s16[8,8,8320]{2,1,0:T(8,128)(2,1)}), s16[8,8,8320]{2,1,0:T(8,128)(2,1)S(1)}, u32[]{:S(2)}, u32[]{:S(2)}) async-start(s16[8,8,8320]{2,1,0:T(8,128)(2,1)} %beamform.1), calls=%async_computation.1 | async-start | bytes 2129920 | tf_op jit(solution)/shard_map/all_to_all | solution.py:396

commit v3 on v2

--- a/solution.py
+++ b/solution.py
@@ -23,6 +23,7 @@
 TILES = BLOCK // LANES
 BEAMS = 4
 DEVICES = 128
+ROWS = 17
 CODE_STEP = 64.0
 LEVELS = 32767.0
 FLOOR = 1e-33
@@ -79,7 +80,13 @@
 FRONT = 136
 
 
-def shift_kernel(delay_ref, v_ref, out_ref, plain_ref, turned_ref):
+def shift_kernel(delay_hbm, v_hbm, out_ref, v_ref, delay_ref, plain_ref, turned_ref, sems):
+    copies = [pltpu.make_async_copy(v_hbm.at[0, p], v_ref.at[p], sems.at[p]) for p in range(2)]
+    copies[0].start()
+    delays = pltpu.make_async_copy(delay_hbm, delay_ref, sems.at[2])
+    delays.start()
+    copies[1].start()
+    delays.wait()
     count = TOTAL // LANES
     lane = lax.broadcasted_iota(jnp.int32, (STA, LANES), 1)
     row = lax.broadcasted_iota(jnp.int32, (STA, LANES), 0)
@@ -90,28 +97,39 @@
     source = lax.broadcasted_iota(jnp.int32, (LANES, LANES), 0)
     target = lax.broadcasted_iota(jnp.int32, (LANES, LANES), 1)
     turn = (target - source) & (LANES - 1)
+    none = jnp.zeros((LANES, LANES), bf16)
+    matrices = []
+    for q in range(0, STA, 2):
+        pair = [(turn == (delay_ref[q + i] & (LANES - 1))).astype(f32).astype(bf16) for i in range(2)]
+        top = jnp.concatenate([pair[0], none], axis=1)
+        low = jnp.concatenate([none, pair[1]], axis=1)
+        matrices.append(jnp.concatenate([top, low], axis=0))
     unroll = 8
     rows = count + 8
     for p in range(2):
         plain = plain_ref.at[p]
         turned = turned_ref.at[p]
+        copies[p].wait()
 
         def fill(i, carry):
             at = pl.multiple_of(i * (unroll * LANES), unroll * LANES)
-            x = v_ref[0, p, :, pl.ds(at, unroll * LANES)].astype(f32)
+            x = v_ref[p, :, pl.ds(at, unroll * LANES)].astype(f32)
             for u in range(unroll):
                 to = pl.multiple_of((FRONT + i * unroll + u) * STA, STA)
                 plain[pl.ds(to, STA), :] = x[:, u * LANES : (u + 1) * LANES]
             return carry
 
-        lax.fori_loop(0, count // unroll, fill, 0)
+        lax.fori_loop(0, count // unroll, fill, 0, unroll=2)
         plain[: FRONT * STA, :] = plain[count * STA : (count + FRONT) * STA, :]
-        for q in range(STA):
-            fine_q = delay_ref[q] & (LANES - 1)
-            coarse_q = lax.shift_right_logical(delay_ref[q], 7)
-            matrix = (turn == fine_q).astype(f32).astype(bf16)
-            x = plain[pl.ds((FRONT - 8 - coarse_q) * STA + q, rows, stride=STA), :].astype(bf16)
-            turned[pl.ds(q, rows, stride=STA), :] = jnp.dot(x, matrix, preferred_element_type=f32)
+        for q in range(0, STA, 2):
+            x = []
+            for i in range(2):
+                coarse = lax.shift_right_logical(delay_ref[q + i], 7)
+                first = (FRONT - 8 - coarse) * STA + q + i
+                x.append(plain[pl.ds(first, rows, stride=STA), :].astype(bf16))
+            y = jnp.dot(jnp.concatenate(x, axis=1), matrices[q // 2], preferred_element_type=f32)
+            for i in range(2):
+                turned[pl.ds(q + i, rows, stride=STA), :] = y[:, i * LANES : (i + 1) * LANES]
 
         def merge(i, before):
             parts = []
@@ -125,7 +143,7 @@
             out_ref[d, p, :, pl.ds(pl.multiple_of(at, unroll * LANES), unroll * LANES)] = wide
             return before
 
-        lax.fori_loop(0, count // unroll, merge, turned[7 * STA : 8 * STA, :])
+        lax.fori_loop(0, count // unroll, merge, turned[7 * STA : 8 * STA, :], unroll=2)
 
 
 def beam_kernel(v_ref, w_ref, out_ref, sums_ref):
@@ -205,7 +223,7 @@
 
 
 def dedisperse_kernel(
-    sub_ref, dm_ref, x_ref, fwd_ref, bwd_ref, end_ref, tw_ref, out_ref, time_ref, base_ref, last_ref
+    dm_ref, x_ref, fwd_ref, bwd_ref, end_ref, tw_ref, out_ref, time_ref, base_ref, last_ref
 ):
     for src in range(STA):
         scale = scale_of(widen(x_ref[src, :, BLOCK:])) * (1.0 / LEVELS)
@@ -219,7 +237,7 @@
 
         lax.fori_loop(0, TILES // 4, decode, 0, unroll=2)
 
-    centre = BASE_FREQ + CHANNEL_WIDTH * (sub_ref[0].astype(f32) + 0.5)
+    centre = BASE_FREQ + CHANNEL_WIDTH * (lax.axis_index("sub").astype(f32) + 0.5)
     row = lax.broadcasted_iota(jnp.int32, (ROOT, ROOT), 0)
     col = lax.broadcasted_iota(jnp.int32, (ROOT, ROOT), 1)
     k1 = 2 * (row & (HALF - 1)) + lax.shift_right_logical(row, 7)
@@ -250,7 +268,7 @@
             u = [v[:, :HALF] + v[:, HALF:] if parity == 0 else v[:, :HALF] - v[:, HALF:] for v in (re, im)]
             u = jnp.concatenate(u, axis=1)
             outs.append(dot_right(u, bwd_ref, parity))
-        measure = DM_STEP * dm_ref[b, 0].astype(f32)
+        measure = DM_STEP * dm_ref[b].astype(f32)
         sums = []
         for parity in range(2):
             at = slice(parity * HALF, (parity + 1) * HALF)
@@ -275,25 +293,26 @@
                 for h in range(2):
                     lanes = slice(h * LANES, (h + 1) * LANES)
                     first = b * 4 + r * 2 + h
-                    last_ref[p, pl.ds(first, 64, stride=16), :] = top[at, lanes]
-                    last_ref[p, pl.ds(64 * 16 + first, 64, stride=16), :] = bottom[at, lanes]
+                    last_ref[p, first, :64] = top[at, lanes]
+                    last_ref[p, first, 64:] = bottom[at, lanes]
 
     def encode(i, carry):
-        for u in range(4):
-            d = i * 4 + u
-            at = pl.ds(pl.multiple_of(d * 16, 16), 16)
-            x = [last_ref[0, at, :], last_ref[1, at, :]]
-            peak = jnp.maximum(jnp.abs(x[0]), jnp.abs(x[1]))
-            peak = jnp.maximum(peak[:8], peak[8:])
-            code = code_of(peak)
-            inverse = LEVELS / scale_of(code)
-            inverse = jnp.concatenate([inverse, inverse], axis=0)
-            for p in range(2):
-                out_ref[d, p * 16 : p * 16 + 16, :] = quantize(x[p], inverse)
-            out_ref[d, 32:40, :] = code.astype(jnp.int32).astype(jnp.int16)
+        at = pl.ds(pl.multiple_of(i * 8, 8), 8)
+        x = [[last_ref[p, k, at, :] for k in range(16)] for p in range(2)]
+        peak = jnp.abs(x[0][0])
+        for k in range(1, 32):
+            peak = jnp.maximum(peak, jnp.abs(x[k // 16][k % 16]))
+        code = code_of(peak)
+        inverse = LEVELS / scale_of(code)
+        first = i * (8 * ROWS)
+        for k in range(16):
+            low = jnp.round(x[0][k] * inverse).astype(jnp.int32) & 0xFFFF
+            high = jnp.round(x[1][k] * inverse).astype(jnp.int32) << 16
+            out_ref[pl.ds(first + k, 8, stride=ROWS), :] = low | high
+        out_ref[pl.ds(first + 16, 8, stride=ROWS), :] = code.astype(jnp.int32)
         return carry
 
-    lax.fori_loop(0, DEVICES // 4, encode, 0)
+    lax.fori_loop(0, DEVICES // 8, encode, 0)
 
 
 SUBS = 4
@@ -306,15 +325,19 @@
     def _():
         power_ref[...] = jnp.zeros_like(power_ref)
 
+    scales = []
+    for sub in range(SUBS):
+        code = x_ref[pl.ds(sub * STA * ROWS + 16, STA, stride=ROWS), :]
+        scales.append(scale_of(code.astype(f32)) * (1.0 / LEVELS))
     for sta in range(STA):
         power = power_ref[sta * 16 : sta * 16 + 16, :]
         for sub in range(SUBS):
-            src = sub * STA + sta
+            src = (sub * STA + sta) * ROWS
             to = sub * 256 + sta * 16
-            scale = scale_of(widen(x_ref[src, 32:40, :])) * (1.0 / LEVELS)
-            scale = jnp.concatenate([scale, scale], axis=0)
-            re = widen(x_ref[src, 0:16, :]) * scale
-            im = widen(x_ref[src, 16:32, :]) * scale
+            scale = jnp.broadcast_to(scales[sub][sta : sta + 1], (16, LANES))
+            both = x_ref[src : src + 16, :]
+            re = ((both << 16) >> 16).astype(f32) * scale
+            im = (both >> 16).astype(f32) * scale
             out_ref[to : to + 16, :] = re
             out_ref[to + 128 : to + 144, :] = im
             power = power + (re * re + im * im)
@@ -327,6 +350,7 @@
 
 VMEM = pl.BlockSpec(memory_space=pltpu.VMEM)
 SMEM = pl.BlockSpec(memory_space=pltpu.SMEM)
+HBM = pl.BlockSpec(memory_space=pltpu.HBM)
 PARAMS = pltpu.CompilerParams(vmem_limit_bytes=48 * 1024 * 1024)
 
 
@@ -334,11 +358,14 @@
     return pl.pallas_call(
         shift_kernel,
         out_shape=jax.ShapeDtypeStruct((STA, 2, STA, BLOCK), bf16),
-        in_specs=[SMEM, VMEM],
+        in_specs=[HBM, HBM],
         out_specs=VMEM,
         scratch_shapes=[
+            pltpu.VMEM((2, STA, TOTAL), bf16),
+            pltpu.SMEM((STA,), jnp.int32),
             pltpu.VMEM((2, (TOTAL // LANES + FRONT) * STA, LANES), f32),
             pltpu.VMEM((2, (TOTAL // LANES + 8) * STA, LANES), f32),
+            pltpu.SemaphoreType.DMA((3,)),
         ],
         compiler_params=PARAMS,
         name="shift",
@@ -357,21 +384,21 @@
     )(volts, weights)
 
 
-def dedisperse(subband, dm_index, coded):
+def dedisperse(dm_index, coded):
     fwd, bwd, end, tw = tables()
     return pl.pallas_call(
         dedisperse_kernel,
-        out_shape=jax.ShapeDtypeStruct((DEVICES, 40, LANES), jnp.int16),
-        in_specs=[SMEM, SMEM] + [VMEM] * 5,
+        out_shape=jax.ShapeDtypeStruct((DEVICES * ROWS, LANES), jnp.int32),
+        in_specs=[SMEM] + [VMEM] * 5,
         out_specs=VMEM,
         scratch_shapes=[
             pltpu.VMEM((TOTAL // LANES, 8, LANES), f32),
             pltpu.VMEM((ROOT, ROOT), f32),
-            pltpu.VMEM((2, DEVICES * 16, LANES), f32),
+            pltpu.VMEM((2, 16, DEVICES, LANES), f32),
         ],
         compiler_params=PARAMS,
         name="dedisperse",
-    )(subband, dm_index, coded, fwd, bwd, end, tw)
+    )(dm_index, coded, fwd, bwd, end, tw)
 
 
 def finish(coded):
@@ -379,7 +406,7 @@
         finish_kernel,
         grid=(16 // SUBS,),
         out_shape=(jax.ShapeDtypeStruct((4096, LANES), f32), jax.ShapeDtypeStruct((128, LANES), f32)),
-        in_specs=[pl.BlockSpec((SUBS * STA, 40, LANES), lambda s: (s, 0, 0))],
+        in_specs=[pl.BlockSpec((SUBS * STA * ROWS, LANES), lambda s: (s, 0))],
         out_specs=(
             pl.BlockSpec((SUBS * 256, LANES), lambda s: (s, 0)),
             pl.BlockSpec((128, LANES), lambda s: (0, 0)),
@@ -394,9 +421,8 @@
     volts = lax.all_to_all(shifted, "sta", 0, 0, tiled=True)
     coded = beamform(volts, beam_weights)
     coded = lax.all_to_all(coded, "sta", 0, 0, tiled=True)
-    subband = lax.axis_index("sub").astype(jnp.int32).reshape(1)
-    coded = dedisperse(subband, dm_index, coded)
-    coded = lax.all_to_all(coded, ("sub", "sta"), 0, 0, tiled=True)
+    coded = dedisperse(dm_index.reshape(BEAMS), coded).reshape(DEVICES, 1, ROWS * LANES)
+    coded = lax.all_to_all(coded, ("sub", "sta"), 0, 0, tiled=True).reshape(DEVICES * ROWS, LANES)
     moved, intensity = finish(coded)
     return moved.reshape(16, 2, 32, 1, 512), intensity.reshape(32, 1, 512)
 

time: 103 us -> 97.9 us (0.950)
  blocking collectives: 65.4 us -> 78.1 us
  waiting for transfers between devices: 11.4 us -> 0 us
  starting transfers between devices: 3.56 us -> 0 us
  Pallas kernels: 19 us -> 16.5 us
    all_to_all x1 -> x2, blocking collectives: 34 us -> 46.7 us  [the longest x1 30.3 us: shards(): lax.all_to_all(coded, ('sub', 'sta'), 0, 0, tiled=True)]
    all_to_all x1 -> x0, waiting for transfers between devices: 11.4 us -> none  [shards(): coded = lax.all_to_all(coded, 'sta', 0, 0, tiled=True)]
    all_to_all x1 -> x0, starting transfers between devices: 3.56 us -> none  [shards(): coded = lax.all_to_all(coded, 'sta', 0, 0, tiled=True)]
    unnamed x17 -> x16, local copies, waits for them, and re-layouts: 2.36 us -> 2.27 us
  transfers between devices with their start and end apart: 1 -> 0, of which waited for: 1 -> 0; matrix products, arithmetic and copies ran while one was open for 0% -> 0% of each run, Pallas kernels for 0% -> 0%
where the time goes in v3:
time: 97.9 us; the launch traced here: 97.7 us
  blocking collectives  78.1 us (80%)
  Pallas kernels  16.5 us (17%)
  local copies, waits for them, and re-layouts  2.27 us (2%)
    all_to_all x1, blocking collectives, shards(): volts = lax.all_to_all(shifted, 'sta', 0, 0, tiled=True)  31.5 us
    all_to_all x1, blocking collectives, shards(): lax.all_to_all(coded, ('sub', 'sta'), 0, 0, tiled=True)  30.3 us
    all_to_all x1, blocking collectives, shards(): coded = lax.all_to_all(coded, 'sta', 0, 0, tiled=True)  16.4 us
    pallas_call x1, Pallas kernels, dedisperse(): pl.pallas_call(dedisperse_kernel, out_shape=jax.ShapeDtypeStruct((DEVICES...  8.81 us
    pallas_call x1, Pallas kernels, shift(): pl.pallas_call(shift_kernel, out_shape=jax.ShapeDtypeStruct((STA, 2, STA,...  3.69 us
    unnamed x16, local copies, waits for them, and re-layouts  2.27 us
    pallas_call x1, Pallas kernels, beamform(): pl.pallas_call(beam_kernel, out_shape=jax.ShapeDtypeStruct((STA, 8, BLOCK...  2.06 us
    pallas_call x1, Pallas kernels, finish(): pl.pallas_call(finish_kernel, grid=(16 // SUBS,), out_shape=(jax.ShapeDty...  1.99 us

profile of v3, /device:TPU:1, one launch (start us, length us, event | category | flops | bytes accessed | tf_op | source)
XLA Modules:
  0.0 97.7 jit_solution(17421575231241224941)
XLA Ops:
  0.6 0.0 copy-start
  0.6 1.6 %copy-done = bf16[1,2,8,65536]{3,2,1,0:T(8,128)(2,1)S(1)} copy-done((bf16[1,2,8,65536]{3,2,1,0:T(8,128)(2,1)S(1)}, bf16[1,2,8,65536]{3,2,1,0:T(8,128)(2,1)}, u32[]{:S(2)}) %copy-start) | copy-done | bytes 2097176
  2.2 0.0 copy-start.6
  2.2 0.7 copy-done.6
  2.9 3.7 %shift.1 = bf16[8,2,8,8192]{3,2,1,0:T(8,128)(2,1)S(1)} custom-call(s32[8]{0:T(128)S(1)} %copy-done.6, bf16[1,2,8,65536]{3,2,1,0:T(8,128)(2,1)S(1)} %copy-done), custom_call_target="tpu_custom_call" | custom-call | tf_op jit(solution)/shard_map/shift/pallas_call | solution.py:358
  6.6 0.0 copy-start.5
  6.6 31.5 %all_to_all.15.v_ref = bf16[8,2,8,8192]{3,2,1,0:T(8,128)(2,1)S(1)} all-to-all(bf16[8,2,8,8192]{3,2,1,0:T(8,128)(2,1)S(1)} %shift.1), channel_id=1, replica_groups=mesh['sub'=16,'sta'=8] {'sta'}, dimensions={0} | all-to-all | bytes 4194304 | tf_op jit(solution)/shard_map/all_to_all | solution.py:421
  38.1 0.0 copy-done.5
  38.1 0.0 copy-start.1
  38.1 0.0 copy-start.2
  38.1 0.0 copy-start.3
  38.1 0.0 copy-start.4
  38.1 0.0 copy-start.7
  38.1 2.1 %beamform.1 = s16[8,8,8320]{2,1,0:T(8,128)(2,1)S(1)} custom-call(bf16[8,2,8,8192]{3,2,1,0:T(8,128)(2,1)S(1)} %all_to_all.15.v_ref, bf16[1,2,32,64]{3,2,1,0:T(8,128)(2,1)S(1)} %copy-done.5), custom_call_target="tpu_custom_call" | custom-call | tf_op jit(solution)/shard_map/beamform/pallas_call | solution.py:376
  40.2 16.4 %all_to_all.16.x_ref = s16[8,8,8320]{2,1,0:T(8,128)(2,1)S(1)} all-to-all(s16[8,8,8320]{2,1,0:T(8,128)(2,1)S(1)} %beamform.1), channel_id=1, replica_groups=mesh['sub'=16,'sta'=8] {'sta'}, dimensions={0} | all-to-all | bytes 2129920 | tf_op jit(solution)/shard_map/all_to_all | solution.py:423
  56.6 0.0 copy-done.1
  56.6 0.0 copy-done.2
  56.6 0.0 copy-done.3
  56.6 0.0 copy-done.4
  56.6 0.0 copy-done.7
  56.6 8.8 %dedisperse.1 = s32[2176,128]{1,0:T(8,128)S(1)} custom-call(s32[4]{0:T(128)S(1)} %bitcast.7, s16[8,8,8320]{2,1,0:T(8,128)(2,1)S(1)} %all_to_all.16.x_ref, bf16[2,2,256,256]{3,2,1,0:T(8,128)(2,1)S(1)} %copy-done.4, bf16[2,2,256,256]{3,2,1,0:T(8,128)(2,1)S(1)} %copy-done.3, bf16[2,2,256,256]{3,2,1,0:T(8,128)(2,1)S(1)} %copy-done.2, f32[2,256,256]{2,1,0:T(8,128)S(1)} %copy-done.1), custom_call_target="tpu_custom_call" | custom-call | tf_op jit(solution)/shard_map/dedisperse/pallas_call | solution.py:389
  65.4 30.3 %all_to_all.17 = s32[128,1,2176]{2,1,0:T(1,128)S(1)} all-to-all(s32[128,1,2176]{2,1,0:T(1,128)S(1)} %bitcast.5), channel_id=1, replica_groups=mesh['sub'=16,'sta'=8] {'sub','sta'}, dimensions={0} | all-to-all | bytes 2228224 | tf_op jit(solution)/shard_map/all_to_all | solution.py:425
  95.7 2.0 %finish.1 = (f32[4096,128]{1,0:T(8,128)}, f32[128,128]{1,0:T(8,128)}) custom-call(s32[2176,128]{1,0:T(8,128)S(1)} %bitcast.6), custom_call_target="tpu_custom_call" | custom-call | tf_op jit(solution)/shard_map/finish/pallas_call | solution.py:405
Async XLA Ops:
  0.6 1.6 %copy-start = (bf16[1,2,8,65536]{3,2,1,0:T(8,128)(2,1)S(1)}, bf16[1,2,8,65536]{3,2,1,0:T(8,128)(2,1)}, u32[]{:S(2)}) copy-start(bf16[1,2,8,65536]{3,2,1,0:T(8,128)(2,1)} %v_hbm.1) | copy-start | bytes 6291460
  2.2 0.7 copy-start.6
  6.6 31.5 %copy-start.5 = (bf16[1,2,32,64]{3,2,1,0:T(8,128)(2,1)S(1)}, bf16[1,2,32,64]{3,2,1,0:T(8,128)(2,1)}, u32[]{:S(2)}) copy-start(bf16[1,2,32,64]{3,2,1,0:T(8,128)(2,1)} %w_ref.1) | copy-start | bytes 24580
  38.1 18.5 %copy-start.1 = (f32[2,256,256]{2,1,0:T(8,128)S(1)}, f32[2,256,256]{2,1,0:T(8,128)}, u32[]{:S(2)}) copy-start(f32[2,256,256]{2,1,0:T(8,128)} %constant.11.clone.tw_ref) | copy-start | bytes 1572868
  38.1 18.5 %copy-start.2 = (bf16[2,2,256,256]{3,2,1,0:T(8,128)(2,1)S(1)}, bf16[2,2,256,256]{3,2,1,0:T(8,128)(2,1)}, u32[]{:S(2)}) copy-start(bf16[2,2,256,256]{3,2,1,0:T(8,128)(2,1)} %constant.10.clone.end_ref) | copy-start | bytes 1572868
  38.1 18.5 %copy-start.3 = (bf16[2,2,256,256]{3,2,1,0:T(8,128)(2,1)S(1)}, bf16[2,2,256,256]{3,2,1,0:T(8,128)(2,1)}, u32[]{:S(2)}) copy-start(bf16[2,2,256,256]{3,2,1,0:T(8,128)(2,1)} %constant.9.clone.bwd_ref) | copy-start | bytes 1572868
  38.1 18.5 %copy-start.4 = (bf16[2,2,256,256]{3,2,1,0:T(8,128)(2,1)S(1)}, bf16[2,2,256,256]{3,2,1,0:T(8,128)(2,1)}, u32[]{:S(2)}) copy-start(bf16[2,2,256,256]{3,2,1,0:T(8,128)(2,1)} %constant.8.clone.fwd_ref) | copy-start | bytes 1572868
  38.1 18.5 %copy-start.7 = (s32[4,1]{0,1:T(1,128)S(1)}, s32[4,1]{0,1:T(1,128)}, u32[]{:S(2)}) copy-start(s32[4,1]{0,1:T(1,128)} %param.11) | copy-start | bytes 52

commit v4 on v3

--- a/solution.py
+++ b/solution.py
@@ -50,7 +50,7 @@
     bwd = fwd.transpose(0, 2, 1)
     order = (2 * np.arange(64)[None, :] + np.arange(2)[:, None]).reshape(-1)
     order = np.concatenate([order, HALF + order])
-    last = bwd[:, order, :]
+    last = bwd[:, order, :] / TOTAL
 
     def pair(t):
         return np.stack(split_np(t), axis=1)
@@ -81,11 +81,15 @@
 
 
 def shift_kernel(delay_hbm, v_hbm, out_ref, v_ref, delay_ref, plain_ref, turned_ref, sems):
-    copies = [pltpu.make_async_copy(v_hbm.at[0, p], v_ref.at[p], sems.at[p]) for p in range(2)]
-    copies[0].start()
-    delays = pltpu.make_async_copy(delay_hbm, delay_ref, sems.at[2])
+    halves_at = [pl.ds(h * (TOTAL // 2), TOTAL // 2) for h in range(2)]
+    delays = pltpu.make_async_copy(delay_hbm, delay_ref, sems.at[4])
     delays.start()
-    copies[1].start()
+    copies = []
+    for p in range(2):
+        for h in range(2):
+            source, to = v_hbm.at[0, p, :, halves_at[h]], v_ref.at[p, :, halves_at[h]]
+            copies.append(pltpu.make_async_copy(source, to, sems.at[p * 2 + h]))
+            copies[-1].start()
     delays.wait()
     count = TOTAL // LANES
     lane = lax.broadcasted_iota(jnp.int32, (STA, LANES), 1)
@@ -106,10 +110,9 @@
         matrices.append(jnp.concatenate([top, low], axis=0))
     unroll = 8
     rows = count + 8
+    steps = count // unroll
     for p in range(2):
         plain = plain_ref.at[p]
-        turned = turned_ref.at[p]
-        copies[p].wait()
 
         def fill(i, carry):
             at = pl.multiple_of(i * (unroll * LANES), unroll * LANES)
@@ -119,31 +122,47 @@
                 plain[pl.ds(to, STA), :] = x[:, u * LANES : (u + 1) * LANES]
             return carry
 
-        lax.fori_loop(0, count // unroll, fill, 0, unroll=2)
-        plain[: FRONT * STA, :] = plain[count * STA : (count + FRONT) * STA, :]
-        for q in range(0, STA, 2):
+        def wrap(i, carry):
+            at = pl.multiple_of((TOTAL - FRONT * LANES) + i * (unroll * LANES), unroll * LANES)
+            x = v_ref[p, :, pl.ds(at, unroll * LANES)].astype(f32)
+            for u in range(unroll):
+                to = pl.multiple_of((i * unroll + u) * STA, STA)
+                plain[pl.ds(to, STA), :] = x[:, u * LANES : (u + 1) * LANES]
+            return carry
+
+        for h in range(2):
+            copies[p * 2 + h].wait()
+            lax.fori_loop(h * steps // 2, (h + 1) * steps // 2, fill, 0, unroll=4)
+        lax.fori_loop(0, FRONT // unroll, wrap, 0, unroll=2)
+    for q in range(0, STA, 2):
+        for p in range(2):
             x = []
             for i in range(2):
                 coarse = lax.shift_right_logical(delay_ref[q + i], 7)
                 first = (FRONT - 8 - coarse) * STA + q + i
-                x.append(plain[pl.ds(first, rows, stride=STA), :].astype(bf16))
+                x.append(plain_ref.at[p][pl.ds(first, rows, stride=STA), :].astype(bf16))
             y = jnp.dot(jnp.concatenate(x, axis=1), matrices[q // 2], preferred_element_type=f32)
             for i in range(2):
-                turned[pl.ds(q + i, rows, stride=STA), :] = y[:, i * LANES : (i + 1) * LANES]
-
-        def merge(i, before):
+                turned_ref.at[p][pl.ds(q + i, rows, stride=STA), :] = y[:, i * LANES : (i + 1) * LANES]
+
+    def merge(i, before):
+        d = i // (TILES // unroll)
+        at = (i % (TILES // unroll)) * (unroll * LANES)
+        last = []
+        for p in range(2):
             parts = []
+            old = before[p]
             for u in range(unroll):
-                now = turned[pl.ds(pl.multiple_of((8 + i * unroll + u) * STA, STA), STA), :]
-                parts.append(jnp.where(keep, now, before))
-                before = now
+                now = turned_ref[p, pl.ds(pl.multiple_of((8 + i * unroll + u) * STA, STA), STA), :]
+                parts.append(jnp.where(keep, now, old))
+                old = now
             wide = jnp.concatenate(parts, axis=1).astype(bf16)
-            d = i // (TILES // unroll)
-            at = (i % (TILES // unroll)) * (unroll * LANES)
             out_ref[d, p, :, pl.ds(pl.multiple_of(at, unroll * LANES), unroll * LANES)] = wide
-            return before
-
-        lax.fori_loop(0, count // unroll, merge, turned[7 * STA : 8 * STA, :], unroll=2)
+            last.append(old)
+        return tuple(last)
+
+    start = tuple(turned_ref[p, 7 * STA : 8 * STA, :] for p in range(2))
+    lax.fori_loop(0, steps, merge, start, unroll=2)
 
 
 def beam_kernel(v_ref, w_ref, out_ref, sums_ref):
@@ -203,13 +222,12 @@
 
 
 QUARTER_HIGH = 1.5703125
-QUARTER_MID = float(np.float32(np.round((np.pi / 2 - QUARTER_HIGH) * 2**22) / 2**22))
-QUARTER_LOW = float(np.float32(np.pi / 2 - QUARTER_HIGH - QUARTER_MID))
+QUARTER_LOW = float(np.float32(np.pi / 2 - QUARTER_HIGH))
 
 
 def cos_sin(phase):
     turns = jnp.round(phase * (2 / np.pi))
-    r = ((phase - turns * QUARTER_HIGH) - turns * QUARTER_MID) - turns * QUARTER_LOW
+    r = (phase - turns * QUARTER_HIGH) - turns * QUARTER_LOW
     quadrant = turns.astype(jnp.int32)
     z = r * r
     s = r + r * z * (-1.6666654611e-1 + z * (8.3321608736e-3 + z * (-1.9515295891e-4)))
@@ -235,7 +253,7 @@
                 time_ref[src * TILES + i * 4 + u] = x[:, u * LANES : (u + 1) * LANES] * scale
             return carry
 
-        lax.fori_loop(0, TILES // 4, decode, 0, unroll=2)
+        lax.fori_loop(0, TILES // 4, decode, 0, unroll=4)
 
     centre = BASE_FREQ + CHANNEL_WIDTH * (lax.axis_index("sub").astype(f32) + 0.5)
     row = lax.broadcasted_iota(jnp.int32, (ROOT, ROOT), 0)
@@ -248,17 +266,19 @@
     base_ref[...] = (TWO_PI * DISPERSION) * offset * offset / (centre * centre * (centre + offset))
 
     flat = time_ref.reshape(TOTAL // LANES * 8, LANES)
-    for b in range(BEAMS):
+    def beam(b):
         x = []
         for p in range(2):
             x.append(
                 jnp.concatenate([flat[pl.ds(h * 8 + p * 4 + b, ROOT, stride=16), :] for h in range(2)], axis=1)
             )
+        yield
         outs = []
         for parity in range(2):
             u = [v[:HALF] + v[HALF:] if parity == 0 else v[:HALF] - v[HALF:] for v in x]
             u = jnp.concatenate(u, axis=0)
             outs.append(dot_left(fwd_ref, parity, u))
+        yield
         re = jnp.concatenate([o[:HALF] for o in outs], axis=0)
         im = jnp.concatenate([o[HALF:] for o in outs], axis=0)
         tw_re, tw_im = tw_ref[0], tw_ref[1]
@@ -268,6 +288,7 @@
             u = [v[:, :HALF] + v[:, HALF:] if parity == 0 else v[:, :HALF] - v[:, HALF:] for v in (re, im)]
             u = jnp.concatenate(u, axis=1)
             outs.append(dot_right(u, bwd_ref, parity))
+        yield
         measure = DM_STEP * dm_ref[b].astype(f32)
         sums = []
         for parity in range(2):
@@ -276,6 +297,7 @@
             y_re, y_im = outs[parity][:, :HALF], outs[parity][:, HALF:]
             u = jnp.concatenate([y_re * c - y_im * s, y_re * s + y_im * c], axis=1)
             sums.append(dot_right(u, fwd_ref, parity))
+        yield
         top, bottom = sums[0] + sums[1], sums[0] - sums[1]
         re = jnp.concatenate([top[:, :HALF], bottom[:, :HALF]], axis=1)
         im = jnp.concatenate([top[:, HALF:], bottom[:, HALF:]], axis=1)
@@ -285,8 +307,8 @@
             at = slice(parity * HALF, (parity + 1) * HALF)
             u = jnp.concatenate([re[at], im[at]], axis=0)
             sums.append(dot_left(end_ref, parity, u))
-        top = (sums[0] + sums[1]) * (1.0 / TOTAL)
-        bottom = (sums[0] - sums[1]) * (1.0 / TOTAL)
+        yield
+        top, bottom = sums[0] + sums[1], sums[0] - sums[1]
         for p in range(2):
             for r in range(2):
                 at = slice(p * HALF + r * 64, p * HALF + r * 64 + 64)
@@ -295,6 +317,12 @@
                     first = b * 4 + r * 2 + h
                     last_ref[p, first, :64] = top[at, lanes]
                     last_ref[p, first, 64:] = bottom[at, lanes]
+
+    running = [beam(b) for b in range(BEAMS)]
+    for tick in range(1 * (BEAMS - 1) + 6):
+        for b in range(BEAMS):
+            if tick >= 1 * b:
+                next(running[b], None)
 
     def encode(i, carry):
         at = pl.ds(pl.multiple_of(i * 8, 8), 8)
@@ -312,7 +340,7 @@
         out_ref[pl.ds(first + 16, 8, stride=ROWS), :] = code.astype(jnp.int32)
         return carry
 
-    lax.fori_loop(0, DEVICES // 8, encode, 0)
+    lax.fori_loop(0, DEVICES // 8, encode, 0, unroll=2)
 
 
 SUBS = 4
@@ -354,6 +382,9 @@
 PARAMS = pltpu.CompilerParams(vmem_limit_bytes=48 * 1024 * 1024)
 
 
+SHIFT_PARAMS = pltpu.CompilerParams(vmem_limit_bytes=50 * 1024 * 1024 + 512 * 1024)
+
+
 def shift(voltages, delays):
     return pl.pallas_call(
         shift_kernel,
@@ -365,9 +396,9 @@
             pltpu.SMEM((STA,), jnp.int32),
             pltpu.VMEM((2, (TOTAL // LANES + FRONT) * STA, LANES), f32),
             pltpu.VMEM((2, (TOTAL // LANES + 8) * STA, LANES), f32),
-            pltpu.SemaphoreType.DMA((3,)),
+            pltpu.SemaphoreType.DMA((5,)),
         ],
-        compiler_params=PARAMS,
+        compiler_params=SHIFT_PARAMS,
         name="shift",
     )(delays, voltages)
 

time: 97.9 us -> 95 us (0.970)
  local copies, waits for them, and re-layouts: 2.27 us -> 0.68 us
  Pallas kernels: 16.5 us -> 15.2 us
    unnamed x16 -> x14, local copies, waits for them, and re-layouts: 2.27 us -> 0.68 us
    pallas_call x1, Pallas kernels: 8.81 us -> 7.62 us  [dedisperse(): pl.pallas_call(dedisperse_kernel, out_shape=jax.ShapeDtypeStruct((DEVICES...]
where the time goes in v4:
time: 95 us; the launch traced here: 94.8 us
  blocking collectives  78.1 us (82%)
  Pallas kernels  15.2 us (16%)
    all_to_all x1, blocking collectives, shards(): volts = lax.all_to_all(shifted, 'sta', 0, 0, tiled=True)  31.5 us
    all_to_all x1, blocking collectives, shards(): lax.all_to_all(coded, ('sub', 'sta'), 0, 0, tiled=True)  30.3 us
    all_to_all x1, blocking collectives, shards(): coded = lax.all_to_all(coded, 'sta', 0, 0, tiled=True)  16.4 us
    pallas_call x1, Pallas kernels, dedisperse(): pl.pallas_call(dedisperse_kernel, out_shape=jax.ShapeDtypeStruct((DEVICES...  7.62 us
    pallas_call x1, Pallas kernels, shift(): pl.pallas_call(shift_kernel, out_shape=jax.ShapeDtypeStruct((STA, 2, STA,...  3.59 us
    pallas_call x1, Pallas kernels, beamform(): pl.pallas_call(beam_kernel, out_shape=jax.ShapeDtypeStruct((STA, 8, BLOCK...  2.06 us
    pallas_call x1, Pallas kernels, finish(): pl.pallas_call(finish_kernel, grid=(16 // SUBS,), out_shape=(jax.ShapeDty...  1.99 us

profile of v4, /device:TPU:1, one launch (start us, length us, event | category | flops | bytes accessed | tf_op | source)
XLA Modules:
  0.0 94.8 jit_solution(16300822657453563210)
XLA Ops:
  0.6 0.0 copy-start.5
  0.6 0.6 copy-done.5
  1.3 3.6 %shift.1 = bf16[8,2,8,8192]{3,2,1,0:T(8,128)(2,1)S(1)} custom-call(s32[8]{0:T(128)S(1)} %copy-done.5, bf16[1,2,8,65536]{3,2,1,0:T(8,128)(2,1)} %v_hbm.1), custom_call_target="tpu_custom_call" | custom-call | tf_op jit(solution)/shard_map/shift/pallas_call | solution.py:389
  4.9 0.0 copy-start.4
  4.9 31.5 %all_to_all.15.v_ref = bf16[8,2,8,8192]{3,2,1,0:T(8,128)(2,1)S(1)} all-to-all(bf16[8,2,8,8192]{3,2,1,0:T(8,128)(2,1)S(1)} %shift.1), channel_id=1, replica_groups=mesh['sub'=16,'sta'=8] {'sta'}, dimensions={0} | all-to-all | bytes 4194304 | tf_op jit(solution)/shard_map/all_to_all | solution.py:452
  36.4 0.0 copy-done.4
  36.4 0.0 copy-start
  36.4 0.0 copy-start.1
  36.4 0.0 copy-start.2
  36.4 0.0 copy-start.3
  36.4 0.0 copy-start.6
  36.4 2.1 %beamform.1 = s16[8,8,8320]{2,1,0:T(8,128)(2,1)S(1)} custom-call(bf16[8,2,8,8192]{3,2,1,0:T(8,128)(2,1)S(1)} %all_to_all.15.v_ref, bf16[1,2,32,64]{3,2,1,0:T(8,128)(2,1)S(1)} %copy-done.4), custom_call_target="tpu_custom_call" | custom-call | tf_op jit(solution)/shard_map/beamform/pallas_call | solution.py:407
  38.5 16.4 %all_to_all.16.x_ref = s16[8,8,8320]{2,1,0:T(8,128)(2,1)S(1)} all-to-all(s16[8,8,8320]{2,1,0:T(8,128)(2,1)S(1)} %beamform.1), channel_id=1, replica_groups=mesh['sub'=16,'sta'=8] {'sta'}, dimensions={0} | all-to-all | bytes 2129920 | tf_op jit(solution)/shard_map/all_to_all | solution.py:454
  54.9 0.0 copy-done
  54.9 0.0 copy-done.1
  54.9 0.0 copy-done.2
  54.9 0.0 copy-done.3
  54.9 0.0 copy-done.6
  54.9 7.6 %dedisperse.1 = s32[2176,128]{1,0:T(8,128)S(1)} custom-call(s32[4]{0:T(128)S(1)} %bitcast.7, s16[8,8,8320]{2,1,0:T(8,128)(2,1)S(1)} %all_to_all.16.x_ref, bf16[2,2,256,256]{3,2,1,0:T(8,128)(2,1)S(1)} %copy-done.3, bf16[2,2,256,256]{3,2,1,0:T(8,128)(2,1)S(1)} %copy-done.2, bf16[2,2,256,256]{3,2,1,0:T(8,128)(2,1)S(1)} %copy-done.1, f32[2,256,256]{2,1,0:T(8,128)S(1)} %copy-done), custom_call_target="tpu_custom_call" | custom-call | tf_op jit(solution)/shard_map/dedisperse/pallas_call | solution.py:420
  62.5 30.3 %all_to_all.17 = s32[128,1,2176]{2,1,0:T(1,128)S(1)} all-to-all(s32[128,1,2176]{2,1,0:T(1,128)S(1)} %bitcast.5), channel_id=1, replica_groups=mesh['sub'=16,'sta'=8] {'sub','sta'}, dimensions={0} | all-to-all | bytes 2228224 | tf_op jit(solution)/shard_map/all_to_all | solution.py:456
  92.8 2.0 %finish.1 = (f32[4096,128]{1,0:T(8,128)}, f32[128,128]{1,0:T(8,128)}) custom-call(s32[2176,128]{1,0:T(8,128)S(1)} %bitcast.6), custom_call_target="tpu_custom_call" | custom-call | tf_op jit(solution)/shard_map/finish/pallas_call | solution.py:436
Async XLA Ops:
  0.6 0.7 copy-start.5
  4.9 31.5 %copy-start.4 = (bf16[1,2,32,64]{3,2,1,0:T(8,128)(2,1)S(1)}, bf16[1,2,32,64]{3,2,1,0:T(8,128)(2,1)}, u32[]{:S(2)}) copy-start(bf16[1,2,32,64]{3,2,1,0:T(8,128)(2,1)} %w_ref.1) | copy-start | bytes 24580
  36.4 18.5 %copy-start = (f32[2,256,256]{2,1,0:T(8,128)S(1)}, f32[2,256,256]{2,1,0:T(8,128)}, u32[]{:S(2)}) copy-start(f32[2,256,256]{2,1,0:T(8,128)} %constant.11.clone.tw_ref) | copy-start | bytes 1572868
  36.4 18.5 %copy-start.1 = (bf16[2,2,256,256]{3,2,1,0:T(8,128)(2,1)S(1)}, bf16[2,2,256,256]{3,2,1,0:T(8,128)(2,1)}, u32[]{:S(2)}) copy-start(bf16[2,2,256,256]{3,2,1,0:T(8,128)(2,1)} %constant.10.clone.end_ref) | copy-start | bytes 1572868
  36.4 18.5 %copy-start.2 = (bf16[2,2,256,256]{3,2,1,0:T(8,128)(2,1)S(1)}, bf16[2,2,256,256]{3,2,1,0:T(8,128)(2,1)}, u32[]{:S(2)}) copy-start(bf16[2,2,256,256]{3,2,1,0:T(8,128)(2,1)} %constant.9.clone.bwd_ref) | copy-start | bytes 1572868
  36.4 18.5 %copy-start.3 = (bf16[2,2,256,256]{3,2,1,0:T(8,128)(2,1)S(1)}, bf16[2,2,256,256]{3,2,1,0:T(8,128)(2,1)}, u32[]{:S(2)}) copy-start(bf16[2,2,256,256]{3,2,1,0:T(8,128)(2,1)} %constant.8.clone.fwd_ref) | copy-start | bytes 1572868
  36.4 18.5 %copy-start.6 = (s32[4,1]{0,1:T(1,128)S(1)}, s32[4,1]{0,1:T(1,128)}, u32[]{:S(2)}) copy-start(s32[4,1]{0,1:T(1,128)} %param.11) | copy-start | bytes 52
